TPU v7x, 32 devices: a 4x4x1 block of a 4x4x8 slice. The times are simulated.
32 devices in a mesh: dp: 1 (over z), fsdp: 32 (over y, x, core).
Axes of the slice: x: 4, y: 4, z: 1, core: 2. Of those that a mesh axis runs over, the one named last changes fastest.
The devices are a block of a 4x4x8 slice.
Arguments:
- hidden: bfloat16 [32, 256, 2048], P(('dp', 'fsdp'))
- doc_lens: int32 [32], P(('dp', 'fsdp'))
- ln_par: float32 [2, 4, 2048], P(None, None, 'fsdp')
- w_qkv: bfloat16 [2, 2048, 16, 384], P(None, 'fsdp')
- b_qkv: bfloat16 [2, 6144], P(None, 'fsdp')
- w_out: bfloat16 [2, 2048, 2048], P(None, 'fsdp')
- b_out: bfloat16 [2, 2048], P(None, 'fsdp')
- w_up: bfloat16 [2, 2048, 8192], P(None, 'fsdp')
- b_up: bfloat16 [2, 8192], P(None, 'fsdp')
- w_down: bfloat16 [2, 8192, 2048], P(None, 'fsdp')
- b_down: bfloat16 [2, 2048], P(None, 'fsdp')
Outputs:
- output: bfloat16 [32, 256, 2048], P(('dp', 'fsdp'))
All inputs are finite; a program needn't handle non-finite values.
Results may differ from a plain program's by a relative error of at most 0.00791475.
Values are sent between devices in bfloat16 or wider.
A program may use at most 768 MiB of HBM per device.

v0:
```python
import jax
import jax.numpy as jnp
from jax import lax
from jax.sharding import PartitionSpec as P

ROPE_BASE = 10000.0
LN_EPS = 1e-5


def layer_norm(row_vals, gain_vec, shift_vec):
    mean_vals = jnp.mean(row_vals, axis=-1, keepdims=True)
    centered = row_vals - mean_vals
    var_vals = jnp.mean(centered * centered, axis=-1, keepdims=True)
    normed = centered * lax.rsqrt(var_vals + LN_EPS)
    return (normed * gain_vec + shift_vec).astype(jnp.bfloat16)


def rotary_tables(seq_len, rot_dim):
    inv_freq = 1.0 / (ROPE_BASE ** (jnp.arange(0, rot_dim, 2, dtype=jnp.float32) / rot_dim))
    angles = jnp.arange(seq_len, dtype=jnp.float32)[:, None] * inv_freq[None, :]
    angles = jnp.concatenate([angles, angles], axis=-1)
    return jnp.cos(angles), jnp.sin(angles)


def apply_rotary(head_vals, cos_tab, sin_tab):
    rot_dim = cos_tab.shape[-1]
    half_rot = rot_dim // 2
    rot_part = head_vals[..., :rot_dim].astype(jnp.float32)
    turned = jnp.concatenate([-rot_part[..., half_rot:], rot_part[..., :half_rot]], axis=-1)
    rotated = rot_part * cos_tab[:, None, :] + turned * sin_tab[:, None, :]
    return jnp.concatenate([rotated.astype(jnp.bfloat16), head_vals[..., rot_dim:]], axis=-1)


def attention_core(qkv_heads, lens_loc):
    num_docs, seq_len, num_heads, triple = qkv_heads.shape
    head_dim = triple // 3
    cos_tab, sin_tab = rotary_tables(seq_len, head_dim // 4)
    queries = apply_rotary(qkv_heads[..., :head_dim], cos_tab, sin_tab)
    keys_rot = apply_rotary(qkv_heads[..., head_dim:2 * head_dim], cos_tab, sin_tab)
    values = qkv_heads[..., 2 * head_dim:]
    scores = jnp.einsum('nqhe,nkhe->nhqk', queries, keys_rot, preferred_element_type=jnp.float32) * (head_dim ** -0.5)
    positions = jnp.arange(seq_len)
    causal = positions[None, :] <= positions[:, None]
    visible = causal[None, None] & (positions[None, None, None, :] < lens_loc[:, None, None, None])
    prob_bf = jax.nn.softmax(jnp.where(visible, scores, -1e30), axis=-1).astype(jnp.bfloat16)
    context = jnp.einsum('nhqk,nkhe->nqhe', prob_bf, values, preferred_element_type=jnp.float32)
    return context.astype(jnp.bfloat16).reshape(num_docs * seq_len, num_heads * head_dim)


def layer_forward(x_loc, lens_loc, ln_full, w_qkv_full, b_qkv_full, w_out_full, b_out_full, w_up_full, b_up_full, w_down_full, b_down_full):
    num_docs, seq_len, d_model = x_loc.shape
    x_rows = x_loc.reshape(num_docs * seq_len, d_model).astype(jnp.float32)
    attn_in = layer_norm(x_rows, ln_full[0], ln_full[1])
    mlp_in = layer_norm(x_rows, ln_full[2], ln_full[3])
    qkv_rows = jnp.dot(attn_in, w_qkv_full.reshape(d_model, -1), preferred_element_type=jnp.float32) + b_qkv_full.astype(jnp.float32)
    qkv_heads = qkv_rows.astype(jnp.bfloat16).reshape(num_docs, seq_len, w_qkv_full.shape[1], w_qkv_full.shape[2])
    context = attention_core(qkv_heads, lens_loc)
    attn_out = jnp.dot(context, w_out_full, preferred_element_type=jnp.float32) + b_out_full.astype(jnp.float32)
    up_rows = jnp.dot(mlp_in, w_up_full, preferred_element_type=jnp.float32) + b_up_full.astype(jnp.float32)
    act_rows = jax.nn.gelu(up_rows, approximate=False).astype(jnp.bfloat16)
    mlp_out = jnp.dot(act_rows, w_down_full, preferred_element_type=jnp.float32) + b_down_full.astype(jnp.float32)
    return (x_rows + attn_out + mlp_out).astype(jnp.bfloat16).reshape(num_docs, seq_len, d_model)


def gather_full(piece, axis_idx):
    return lax.all_gather(piece, 'fsdp', axis=axis_idx, tiled=True)


def solution(mesh):
    row_spec = P(('dp', 'fsdp'), None, None)
    in_specs = (row_spec, P(('dp', 'fsdp')), P(None, None, 'fsdp'), P(None, 'fsdp', None, None), P(None, 'fsdp'), P(None, 'fsdp', None), P(None, 'fsdp'), P(None, 'fsdp', None), P(None, 'fsdp'), P(None, 'fsdp', None), P(None, 'fsdp'))

    def local_step(hidden_loc, lens_loc, ln_par, w_qkv, b_qkv, w_out, b_out, w_up, b_up, w_down, b_down):
        x_loc = hidden_loc
        for layer_idx in range(ln_par.shape[0]):
            ln_full = gather_full(ln_par[layer_idx], 1)
            w_qkv_full = gather_full(w_qkv[layer_idx], 0)
            b_qkv_full = gather_full(b_qkv[layer_idx], 0)
            w_out_full = gather_full(w_out[layer_idx], 0)
            b_out_full = gather_full(b_out[layer_idx], 0)
            w_up_full = gather_full(w_up[layer_idx], 0)
            b_up_full = gather_full(b_up[layer_idx], 0)
            w_down_full = gather_full(w_down[layer_idx], 0)
            b_down_full = gather_full(b_down[layer_idx], 0)
            x_loc = layer_forward(x_loc, lens_loc, ln_full, w_qkv_full, b_qkv_full, w_out_full, b_out_full, w_up_full, b_up_full, w_down_full, b_down_full)
        return x_loc

    return jax.shard_map(local_step, mesh=mesh, in_specs=in_specs, out_specs=row_spec, check_vma=False)
```

profile of v0, /device:TPU:97, one launch (start us, length us, event | category | flops | bytes accessed | tf_op | source)
XLA Modules:
  0.0 754.9 jit_solution(4958439292992388731)
XLA Ops:
  6.6 2.8 slice_bitcast_fusion.2
  11.3 1.5 fusion.329
  12.9 3.1 fusion.330
  19.9 52.1 %all-reduce.6 = (bf16[6144]{0:T(1024)(128)(2,1)S(1)}, bf16[2048]{0:T(1024)(128)(2,1)S(1)}, bf16[2048]{0:T(1024)(128)(2,1)S(1)}, bf16[6144]{0:T(1024)(128)(2,1)S(...) all-reduce(bf16[6144]{0:T(1024)(128)(2,1)S(1)} %dynamic-update-slic, ...), channel_id=4, replica_groups=mesh['dp'=1,'fsdp'=32] {'fsdp'}, use_global_device_ids=true, to_apply=%add | all-reduce | flops 20480 | bytes 81920
  73.2 27.8 %all-gather.6 = bf16[1,8192]{1,0:T(2,128)(2,1)S(1)} all-gather(bf16[1,256]{1,0:T(2,128)(2,1)S(1)} %get-tuple-element.50), channel_id=8, replica_groups=mesh['dp'=1,'fsdp'=32] {'fsdp'}, dimensions={1}, use_global_device_ids=true | all-gather | bytes 16896 | tf_op jit(solution)/shard_map/all_gather | solution.py:66
  101.1 32.0 %all-gather.15 = bf16[1,8192]{1,0:T(2,128)(2,1)S(1)} all-gather(bf16[1,256]{1,0:T(2,128)(2,1)S(1)} %get-tuple-element.49), channel_id=17, replica_groups=mesh['dp'=1,'fsdp'=32] {'fsdp'}, dimensions={1}, use_global_device_ids=true | all-gather | bytes 16896 | tf_op jit(solution)/shard_map/all_gather | solution.py:66
  135.6 37.4 %all-gather = f32[1,4,2048]{1,0,2:T(1,128)S(1)} all-gather(f32[1,4,64]{1,0,2:T(1,128)S(1)} %copy.112), channel_id=2, replica_groups=mesh['dp'=1,'fsdp'=32] {'fsdp'}, dimensions={2}, use_global_device_ids=true | all-gather | bytes 33792 | tf_op jit(solution)/shard_map/all_gather | solution.py:66
  173.0 32.6 %all-gather.9 = f32[1,4,2048]{1,0,2:T(1,128)S(1)} all-gather(f32[1,4,64]{1,0,2:T(1,128)S(1)} %copy.119), channel_id=11, replica_groups=mesh['dp'=1,'fsdp'=32] {'fsdp'}, dimensions={2}, use_global_device_ids=true | all-gather | bytes 33792 | tf_op jit(solution)/shard_map/all_gather | solution.py:66
  206.5 43.0 %slice_reduce_fusion.5 = (f32[2048]{0:T(1024)S(1)}, f32[2048]{0:T(1024)S(1)}, f32[2048]{0:T(1024)S(1)}, f32[2048]{0:T(1024)S(1)}) fusion(f32[1,4,2048]{1,0,2:T(1,128)S(1)} %all-gather), kind=kLoop, calls=%fused_computation.197 | loop fusion | bytes 65536 | tf_op jit(solution)/shard_map/slice | solution.py:54
  249.5 43.4 %slice_reduce_fusion.1 = (f32[2048]{0:T(1024)}, f32[2048]{0:T(1024)}, f32[2048]{0:T(1024)}, f32[2048]{0:T(1024)}) fusion(f32[1,4,2048]{1,0,2:T(1,128)S(1)} %all-gather.9), kind=kLoop, calls=%fused_computation.192 | loop fusion | bytes 65536 | tf_op jit(solution)/shard_map/slice | solution.py:54
  292.9 25.7 %copy.125 = bf16[256,8,16,384]{3,1,2,0:T(8,128)(2,1)} copy(bf16[256,8,16,384]{3,2,1,0:T(8,128)(2,1)} %bitcast.172) | data formatting | bytes 50331648
  318.6 11.8 %fusion.40 = bf16[256,6144]{1,0:T(8,128)(2,1)S(1)} fusion(bf16[2048,6144]{1,0:T(8,128)(2,1)} %bitcast.174, f32[6144]{0:T(1024)S(1)} %convert_element_type.163, bf16[1,256,2048]{2,1,0:T(8,128)(2,1)S(1)} %copy-done, f32[2048]{0:T(1024)S(1)} %get-tuple-element.10, f32[2048]{0:T(1024)S(1)} %get-tuple-element.11, f32[256]{0:T(256)S(1)} %add_rsqrt_fusion.1, ...), kind=kOutput, calls=%fused_computation.56 | convolution fusion | flops 6448742400 | bytes 29403136 | tf_op jit(solution)/shard_map/dot_general | solution.py:55
  331.1 1.2 slice.198
  332.9 1.2 copy.116
  334.2 1.3 copy.118
  335.4 2.4 copy.114
  337.8 25.5 %copy.127 = bf16[256,8,16,384]{3,1,2,0:T(8,128)(2,1)} copy(bf16[256,8,16,384]{3,2,1,0:T(8,128)(2,1)} %bitcast.171) | data formatting | bytes 50331648
  365.7 1.4 fusion.199
  367.2 1.3 fusion.221
  368.5 1.5 fusion.334
  370.0 1.4 fusion.213
  371.5 6.1 fusion.144
  377.6 31.7 %fusion.169.clone.4 = bf16[256,8192]{1,0:T(8,128)(2,1)} fusion(bf16[1,2048,8192]{2,1,0:T(8,128)(2,1)} %all-gather.31.cloned.1.call-done, f32[8192]{0:T(1024)S(1)} %bitcast.185, bf16[1,256,2048]{2,1,0:T(8,128)(2,1)S(1)} %copy-done.1, f32[2048]{0:T(1024)S(1)} %get-tuple-element.12, ...), kind=kOutput, calls=%fused_computation.16.clone.clone.clone.clone.clone.clone.clone.clone.clone.clone.1 | convolution fusion | flops 8731492352 | bytes 38848512 | tf_op jit(solution)/shard_map/dot_general | solution.py:59
  409.3 53.5 %all-gather.33.cloned.1.call-done = bf16[1,8192,2048]{2,1,0:T(8,128)(2,1)} async-done(((bf16[1,256,2048]{2,1,0:T(8,128)(2,1)}), bf16[1,8192,2048]{2,1,0:T(8,128)(2,1)}) %all-gather.33.cloned.1.call-update) | async-done | bytes 33554448 | tf_op jit(solution)/shard_map/all_gather | solution.py:66
  462.8 16.8 %convert_reduce_fusion = (f32[256]{0:T(256)S(1)}, bf16[256,2048]{1,0:T(8,128)(2,1)S(1)}) fusion(f32[256,2048]{1,0:T(8,128)S(1)} %fusion.144, f32[2048]{0:T(1024)S(1)} %convert_element_type.165, bf16[1,8192,2048]{2,1,0:T(8,128)(2,1)} %all-gather.33.cloned.1.call-done, bf16[256,8192]{1,0:T(8,128)(2,1)} %fusion.169.clone.4), kind=kOutput, calls=%fused_computation.130 | convolution fusion | flops 8592556032 | bytes 40903680 | tf_op jit(solution)/shard_map/dot_general | solution.py:61
  480.6 13.0 %fusion.41 = bf16[256,6144]{1,0:T(8,128)(2,1)} fusion(bf16[2048,6144]{1,0:T(8,128)(2,1)} %bitcast.173, f32[6144]{0:T(1024)S(1)} %copy-done.17, bf16[256,2048]{1,0:T(8,128)(2,1)S(1)} %get-tuple-element.58, f32[2048]{0:T(1024)S(1)} %copy-done.20, f32[2048]{0:T(1024)S(1)} %copy-done.21, f32[256]{0:T(256)S(1)} %add_rsqrt_fusion, f32[256]{0:T(256)S(1)} %broadcast_multiply_fusion), kind=kOutput, calls=%fused_computation.57 | convolution fusion | flops 6448742400 | bytes 29403136 | tf_op jit(solution)/shard_map/dot_general | solution.py:55
  493.5 3.2 copy.104
  496.7 0.9 fusion.325
  497.6 0.9 copy-done.2
  498.6 1.5 copy.121
  500.0 1.5 convert_element_type.141
  501.6 1.6 slice.214
  503.7 1.5 convert_element_type.143
  505.2 1.6 slice.218
  506.8 1.3 fusion.326
  508.0 1.6 copy.122
  509.6 2.4 copy.124
  512.0 2.3 slice_negate_fusion
  514.3 2.2 slice_negate_fusion.1
  516.6 1.4 fusion.203
  518.0 1.3 fusion.226
  519.3 1.2 fusion.339
  520.6 2.8 fusion.212
  523.4 6.1 convert_add_fusion
  529.5 91.7 %all-gather.39.cloned.1.call-done = bf16[1,2048,8192]{2,1,0:T(8,128)(2,1)} async-done(((bf16[1,64,8192]{2,1,0:T(8,128)(2,1)}), bf16[1,2048,8192]{2,1,0:T(8,128)(2,1)}) %all-gather.39.cloned.1.call-update) | async-done | bytes 33554448 | tf_op jit(solution)/shard_map/all_gather | solution.py:66
  621.2 32.0 %fusion.360 = bf16[256,8192]{1,0:T(8,128)(2,1)} fusion(bf16[1,2048,8192]{2,1,0:T(8,128)(2,1)} %all-gather.39.cloned.1.call-done, f32[8192]{0:T(1024)S(1)} %bitcast.184, bf16[256,2048]{1,0:T(8,128)(2,1)S(1)} %copy-done.7, f32[2048]{0:T(1024)S(1)} %copy-done.19, f32[2048]{0:T(1024)S(1)} %copy-done.18, ...), kind=kOutput, calls=%fused_computation.19.clone.clone.clone.clone.clone.clone.clone.clone.clone.clone.1 | convolution fusion | flops 8731492352 | bytes 38848512 | tf_op jit(solution)/shard_map/dot_general | solution.py:59
  653.2 77.6 %all-gather.41.cloned.1.call-done = bf16[1,8192,2048]{2,1,0:T(8,128)(2,1)} async-done(((bf16[1,256,2048]{2,1,0:T(8,128)(2,1)}), bf16[1,8192,2048]{2,1,0:T(8,128)(2,1)}) %all-gather.41.cloned.1.call-update) | async-done | bytes 33554448 | tf_op jit(solution)/shard_map/all_gather | solution.py:66
  730.8 17.0 %fusion.174 = bf16[1,256,2048]{2,1,0:T(8,128)(2,1)} fusion(f32[256,2048]{1,0:T(8,128)S(1)} %convert_add_fusion, bf16[1,8192,2048]{2,1,0:T(8,128)(2,1)} %all-gather.41.cloned.1.call-done, f32[2048]{0:T(1024)S(1)} %copy-done.22, bf16[256,8192]{1,0:T(8,128)(2,1)} %fusion.360), kind=kOutput, calls=%fused_computation.148 | convolution fusion | flops 8591507456 | bytes 40902656 | tf_op jit(solution)/shard_map/dot_general | solution.py:61
  (125 shorter events, 14.8 us)
Async XLA Ops:
  6.5 3.8 copy-start.14
  6.5 4.7 copy-start.11
  6.6 286.4 %all-gather.27.cloned.1.call-start = ((), (), s32[]{:S(2)}) async-start(), calls=%async_computation | async-start | bytes 25952256 | tf_op jit(solution)/shard_map/all_gather | solution.py:66
  9.4 328.4 %all-gather.35.cloned.1.call-start = ((), (), s32[]{:S(2)}) async-start(), calls=%async_computation.4 | async-start | bytes 25952256 | tf_op jit(solution)/shard_map/all_gather | solution.py:66
  10.2 361.2 %all-gather.29.cloned.1.call-start = ((), (), s32[]{:S(2)}) async-start(), calls=%async_computation.1 | async-start | bytes 8650752 | tf_op jit(solution)/shard_map/all_gather | solution.py:66
  11.2 366.3 %all-gather.31.cloned.1.call-start = ((), (), s32[]{:S(2)}) async-start(), calls=%async_computation.2 | async-start | bytes 34603008 | tf_op jit(solution)/shard_map/all_gather | solution.py:66
  12.8 5.6 copy-start.26
  12.8 5.9 copy-start.27
  12.8 6.6 copy-start.23
  12.8 59.2 %copy-start.24 = (f32[2,4,64]{2,1,0:T(4,128)S(1)}, f32[2,4,64]{2,1,0:T(4,128)}, u32[]{:S(2)}) copy-start(f32[2,4,64]{2,1,0:T(4,128)} %param.13) | copy-start | bytes 6148
  12.9 60.3 %copy-start.25 = (bf16[2,256]{1,0:T(2,128)(2,1)S(1)}, bf16[2,256]{1,0:T(2,128)(2,1)}, u32[]{:S(2)}) copy-start(bf16[2,256]{1,0:T(2,128)(2,1)} %param.19) | copy-start | bytes 3076
  12.9 449.9 %all-gather.33.cloned.1.call-start = ((), (), s32[]{:S(2)}) async-start(), calls=%async_computation.3 | async-start | bytes 34603008 | tf_op jit(solution)/shard_map/all_gather | solution.py:66
  16.1 189.6 %copy-start = (bf16[1,256,2048]{2,1,0:T(8,128)(2,1)S(1)}, bf16[1,256,2048]{2,1,0:T(8,128)(2,1)}, u32[]{:S(2)}) copy-start(bf16[1,256,2048]{2,1,0:T(8,128)(2,1)} %param.11) | copy-start | bytes 3145732
  16.1 507.2 %all-gather.37.cloned.1.call-start = ((), (), s32[]{:S(2)}) async-start(), calls=%async_computation.5 | async-start | bytes 8650752 | tf_op jit(solution)/shard_map/all_gather | solution.py:66
  16.8 604.4 %all-gather.39.cloned.1.call-start = ((), (), s32[]{:S(2)}) async-start(), calls=%async_computation.6 | async-start | bytes 34603008 | tf_op jit(solution)/shard_map/all_gather | solution.py:66
  17.6 713.2 %all-gather.41.cloned.1.call-start = ((), (), s32[]{:S(2)}) async-start(), calls=%async_computation.7 | async-start | bytes 34603008 | tf_op jit(solution)/shard_map/all_gather | solution.py:66
  365.7 1.5 copy-start.9
  365.7 1.5 copy-start.10
  368.5 1.5 copy-start.12
  370.0 1.5 copy-start.1
  409.3 71.3 %copy-start.17 = (f32[6144]{0:T(1024)S(1)}, f32[6144]{0:T(1024)}, u32[]{:S(2)}) copy-start(f32[6144]{0:T(1024)} %convert_element_type.166) | copy-start | bytes 73732
  409.3 71.3 %copy-start.20 = (f32[2048]{0:T(1024)S(1)}, f32[2048]{0:T(1024)}, u32[]{:S(2)}) copy-start(f32[2048]{0:T(1024)} %get-tuple-element.6) | copy-start | bytes 24580
  409.3 71.3 %copy-start.21 = (f32[2048]{0:T(1024)S(1)}, f32[2048]{0:T(1024)}, u32[]{:S(2)}) copy-start(f32[2048]{0:T(1024)} %get-tuple-element.7) | copy-start | bytes 24580
  479.6 1.0 copy-start.6
  496.7 1.8 copy-start.2
  498.6 4.6 copy-start.13
  503.6 3.1 copy-start.3
  512.0 4.6 copy-start.4
  512.0 4.6 copy-start.5
  516.6 1.4 copy-start.8
  520.5 2.8 copy-start.7
  520.5 2.8 copy-start.15
  523.4 97.8 %copy-start.16 = (f32[1,8192]{1,0:T(1,128)S(1)}, f32[1,8192]{1,0:T(1,128)}, u32[]{:S(2)}) copy-start(f32[1,8192]{1,0:T(1,128)} %convert_element_type.161) | copy-start | bytes 98308
  523.4 97.8 %copy-start.18 = (f32[2048]{0:T(1024)S(1)}, f32[2048]{0:T(1024)}, u32[]{:S(2)}) copy-start(f32[2048]{0:T(1024)} %get-tuple-element.5) | copy-start | bytes 24580
  523.4 97.8 %copy-start.19 = (f32[2048]{0:T(1024)S(1)}, f32[2048]{0:T(1024)}, u32[]{:S(2)}) copy-start(f32[2048]{0:T(1024)} %get-tuple-element.8) | copy-start | bytes 24580
  621.2 109.6 %copy-start.22 = (f32[2048]{0:T(1024)S(1)}, f32[2048]{0:T(1024)}, u32[]{:S(2)}) copy-start(f32[2048]{0:T(1024)} %convert_element_type.168) | copy-start | bytes 24580
Sparse Core Ops, SparseCore 0:
  9.6 92.5 all-gather.26
  104.2 90.2 all-gather.34
  196.6 47.0 all-gather.28
  245.6 107.7 all-gather.30
  355.3 107.4 all-gather.32
  464.7 46.5 all-gather.36
  513.4 107.7 all-gather.38
  623.3 107.4 all-gather.40
where the time goes:
time: 763 us; the launch traced here: 755 us
  waiting for transfers between devices  226 us (30%)
  blocking collectives  182 us (24%)
  local copies, waits for them, and re-layouts  172 us (23%)
  matrix products  141 us (18%)
  other arithmetic  18.9 us (2%)
  between operations  14.9 us (2%)
    all_gather x8, waiting for transfers between devices, gather_full(): return lax.all_gather(piece, 'fsdp', axis=axis_idx, tiled=True)  223 us
    all_gather x4, blocking collectives, gather_full(): return lax.all_gather(piece, 'fsdp', axis=axis_idx, tiled=True)  130 us
    slice x2, local copies, waits for them, and re-layouts, layer_forward(): mlp_in = layer_norm(x_rows, ln_full[2], ln_full[3])  86.5 us
    unnamed x83, local copies, waits for them, and re-layouts  68.8 us
    dot_general x2, matrix products, layer_forward(): jnp.dot(mlp_in, w_up_full, preferred_element_type=jnp.float32)  63.7 us
    unnamed x1, blocking collectives  52.1 us
    dot_general x2, matrix products, layer_forward(): jnp.dot(act_rows, w_down_full, preferred_element_type=jnp.float32)  33.8 us
    dot_general x2, matrix products, layer_forward(): jnp.dot(attn_in, w_qkv_full.reshape(d_model, -1), preferred_element_type=...  24.7 us
  transfers between devices with their start and end apart: 8, of which 3 were waited for; matrix products, arithmetic and copies ran while one was open for 41% of the time, Pallas kernels for 0%

commit v1 on v0

v1 whole, which is shorter than its diff:
```python
import functools
import math

import jax
import jax.numpy as jnp
import numpy as np
from jax import lax
from jax.experimental import pallas as pl
from jax.experimental.pallas import tpu as pltpu
from jax.sharding import PartitionSpec as P

ROPE_BASE = 10000.0
LN_EPS = 1e-5
CORES = 2
MESH = pl.DeviceIdType.MESH


def rotary_factors(seq_len, head_dim):
    rot = head_dim // 4
    half = rot // 2
    inv_freq = (1.0 / (ROPE_BASE ** (np.arange(0, rot, 2, dtype=np.float32) / rot))).astype(np.float32)
    angles = np.arange(seq_len, dtype=np.float32)[:, None] * inv_freq[None, :]
    cos, sin = np.cos(angles), np.sin(angles)
    out = np.zeros((3, seq_len, head_dim), np.float32)
    out[0] = 1.0
    out[0, :, :half], out[0, :, half:rot] = cos, cos
    out[1, :, :half] = -sin
    out[2, :, half:rot] = sin
    return jnp.asarray(out)


def send(src, dst, send_sem, recv_sem, dev):
    pltpu.make_async_remote_copy(src_ref=src, dst_ref=dst, send_sem=send_sem, recv_sem=recv_sem, device_id={"fsdp": dev}, device_id_type=MESH).start()


def settle(ref, sem):
    pltpu.make_async_copy(ref, ref, sem).wait()


class Place:
    def __init__(self, side):
        me = lax.axis_index("fsdp")
        self.side, self.me = side, me
        self.core = lax.rem(me, CORES)
        self.chip = me // CORES
        self.col = lax.rem(self.chip, side)
        self.row = self.chip // side
        self.sib = self.dev(self.row, self.col, 1 - self.core)

    def dev(self, row, col, core):
        return (row * self.side + col) * CORES + core

    def step(self, pos, by):
        return lax.rem(pos + by + self.side, self.side)

    def in_row(self, by):
        return self.dev(self.row, self.step(self.col, by), self.core)

    def in_col(self, by):
        return self.dev(self.step(self.row, by), self.col, self.core)


class Ring:
    def __init__(self, place, pos, right, left, blk, own, ss, rs):
        self.pos, self.right, self.left, self.blk, self.own, self.ss, self.rs = pos, right, left, blk, own, ss, rs
        self.prev, self.next, self.far = place.step(pos, -1), place.step(pos, 1), place.step(pos, 2)

    def _send(self, src, pos, half, i, j, dev):
        send(src, self.blk(pos, half), self.ss.at[i], self.rs.at[j], dev)

    def start(self):
        self._send(self.own(0), self.pos, 0, 0, 0, self.right)
        self._send(self.own(1), self.pos, 1, 2, 3, self.left)
        self._send(self.own(1), self.pos, 1, 1, 1, self.right)
        self._send(self.own(0), self.pos, 0, 3, 2, self.left)

    def forward(self):
        settle(self.blk(self.prev, 0), self.rs.at[0])
        self._send(self.blk(self.prev, 0), self.prev, 0, 4, 4, self.right)
        settle(self.blk(self.next, 1), self.rs.at[3])
        self._send(self.blk(self.next, 1), self.next, 1, 5, 5, self.left)

    def rest(self):
        settle(self.blk(self.prev, 1), self.rs.at[1])
        settle(self.blk(self.next, 0), self.rs.at[2])

    def last(self):
        settle(self.blk(self.far, 0), self.rs.at[4])
        settle(self.blk(self.far, 1), self.rs.at[5])

    def drain(self):
        for i, half in enumerate((0, 1, 1, 0, 0, 1)):
            settle(self.blk(self.pos, half), self.ss.at[i])


class Gather:
    def __init__(self, place, blk, own, ss, rs, cs, cr):
        mine = lambda row, half: blk(row, half, place.core)
        self.theirs = lambda row, half: blk(row, half, 1 - place.core)
        own = own if own is not None else (lambda half: mine(place.row, half))
        self.ring = Ring(place, place.row, place.in_col(1), place.in_col(-1), mine, own, ss, rs)
        self.sib, self.cs, self.cr = place.sib, cs, cr
        self.blocks = (self.ring.pos, self.ring.prev, self.ring.next, self.ring.far)

    def give(self, rel, half, src=None):
        i = rel * 2 + half
        blk = self.ring.blk(self.blocks[rel], half)
        send(blk if src is None else src, blk, self.cs.at[i], self.cr.at[i], self.sib)

    def start(self):
        self.ring.start()
        self.give(0, 0, self.ring.own(0))
        self.give(0, 1, self.ring.own(1))

    def forward(self):
        self.ring.forward()
        self.give(1, 0)
        self.give(2, 1)

    def finish(self):
        self.ring.rest()
        self.give(1, 1)
        self.give(2, 0)
        self.ring.last()
        self.give(3, 0)
        self.give(3, 1)
        for rel in range(4):
            for half in range(2):
                settle(self.theirs(self.blocks[rel], half), self.cr.at[rel * 2 + half])

    def drain(self):
        self.ring.drain()
        for rel in range(4):
            for half in range(2):
                settle(self.ring.blk(self.blocks[rel], half), self.cs.at[rel * 2 + half])


def weight_gathers(place, bufs, wo_own, wd_own, sems):
    wq, wu, wo, wd = bufs
    cols = wq.shape[1] // 2
    o_rows, d_rows = wo.shape[2] // 2, wd.shape[2] // 2
    specs = (
        (lambda row, half, core: wq.at[row, pl.ds(half * cols, cols), core], None),
        (lambda row, half, core: wu.at[row, pl.ds(half * cols, cols), core], None),
        (lambda row, half, core: wo.at[row, core, pl.ds(half * o_rows, o_rows)], lambda half: wo_own.at[pl.ds(half * o_rows, o_rows)]),
        (lambda row, half, core: wd.at[row, core, pl.ds(half * d_rows, d_rows)], lambda half: wd_own.at[pl.ds(half * d_rows, d_rows)]),
    )
    return [Gather(place, blk, own, *(s.at[t] for s in sems)) for t, (blk, own) in enumerate(specs)]


def both_layers(side, x_ref, vec_ref, bias_ref, rot_ref, wq_ref, wu_ref, wo_ref, wd_ref,
                out_ref, wq1, wu1, wo1, wd1,
                wq, wu, wo, wd, xg, xg1, a_buf, act, ctx, part, hop_a, hop_b, fin, vec_in, bias_in, vec, bq, bu,
                v_ss, v_rs, b_ss, b_rs, x_ss, x_rs, a_ss, a_rs, w_ss, w_rs, c_ss, c_rs, r_ss, r_rs, loc, loc1):
    f32, bf = jnp.float32, jnp.bfloat16
    place = Place(side)
    count = side * side * CORES
    seq, d_model = x_ref.shape
    head = rot_ref.shape[2]
    triple = 3 * head
    per = side
    ff = act.shape[2]
    half = seq // 2
    wide = wu_ref.shape[2] // (side * side)
    right, left = place.in_row(1), place.in_row(-1)
    nxt, prv, far = place.step(place.col, 1), place.step(place.col, -1), place.step(place.col, 2)

    barrier = pltpu.get_barrier_semaphore()
    others = [lax.rem(place.me + d, count) for d in range(1, count)]
    for dev in others:
        pl.semaphore_signal(barrier, inc=1, device_id={"fsdp": dev}, device_id_type=MESH)
    pl.semaphore_wait(barrier, count - 1)

    def exchange(layer, kind, dst_buf):
        for d in (1, 3, 2, 0):
            col = place.step(place.col, d)
            dst = dst_buf.at[place.row, place.col, place.core]
            pairs = [(wq_ref.at[layer, col], dst)]
            if kind:
                pairs = []
                for k in range(side):
                    off = pl.multiple_of((k * side + col) * wide, wide)
                    pairs.append((wu_ref.at[layer, :, pl.ds(off, wide)], dst.at[:, pl.ds(k * wide, wide)]))
            for src, to in pairs:
                if d:
                    send(src, to, a_ss.at[layer, kind, d], a_rs.at[layer, kind, d], place.in_row(d))
                else:
                    pltpu.make_async_copy(src, to, a_rs.at[layer, kind, d]).start()

    def exchanged(layer, kind, dst_buf):
        for d in range(side):
            settle(dst_buf.at[place.row, place.step(place.col, -d), place.core], a_rs.at[layer, kind, d])

    gathers = [
        weight_gathers(place, (wq, wu, wo, wd), wo_ref.at[0], wd_ref.at[0], [s.at[0] for s in (w_ss, w_rs, c_ss, c_rs)]),
        weight_gathers(place, (wq1, wu1, wo1, wd1), wo_ref.at[1], wd_ref.at[1], [s.at[1] for s in (w_ss, w_rs, c_ss, c_rs)]),
    ]
    gq, gu, go, gd = gathers[0]
    gq1, gu1, go1, gd1 = gathers[1]
    rows_of = lambda ref, col, h: ref.at[col, pl.ds(h * half, half)]
    x_ring = Ring(place, place.col, right, left, lambda col, h: rows_of(xg, col, h), lambda h: x_ref.at[pl.ds(h * half, half)], x_ss.at[0], x_rs.at[0])
    x1_ring = Ring(place, place.col, right, left, lambda col, h: rows_of(xg1, col, h), lambda h: rows_of(xg1, place.col, h), x_ss.at[1], x_rs.at[1])

    exchange(0, 0, wq)
    vec_at = lambda core, chip: vec_in.at[core, :, pl.ds(pl.multiple_of(chip * head, head), head)]
    bias_at = lambda core, row: bias_in.at[core, :, pl.ds(pl.multiple_of(row * head, head), head)]
    for d, dev in enumerate(others):
        send(vec_ref, vec_at(place.core, place.chip), v_ss.at[d], v_rs.at[d], dev)
    column = [(e, c) for e in range(side) for c in range(CORES) if e or c]
    for i, (e, c) in enumerate(column):
        dev = place.dev(place.step(place.row, e), place.col, lax.rem(place.core + c, CORES))
        send(bias_ref, bias_at(place.core, place.row), b_ss.at[i], b_rs.at[i], dev)
    exchange(0, 1, wu)
    go.start()
    x_ring.start()
    own = [(x_ref, xg.at[place.col]), (wo_ref.at[0], wo.at[place.row, place.core]), (wd_ref.at[0], wd.at[place.row, place.core]),
           (wo_ref.at[1], wo1.at[place.row, place.core]), (wd_ref.at[1], wd1.at[place.row, place.core])]
    for i, (src, dst) in enumerate(own):
        pltpu.make_async_copy(src, dst, loc.at[i]).start()

    vec_in[place.core, :, pl.ds(pl.multiple_of(place.chip * head, head), head)] = vec_ref[...]
    bias_in[place.core, :, pl.ds(pl.multiple_of(place.row * head, head), head)] = bias_ref[...]

    exchanged(0, 0, wq)
    gq.start()
    exchanged(0, 1, wu)
    gu.start()

    for d in range(1, count):
        src = lax.rem(place.me + count - d, count)
        settle(vec_at(lax.rem(src, CORES), src // CORES), v_rs.at[d - 1])
    for i, (e, c) in enumerate(column):
        settle(bias_at(lax.rem(place.core + c, CORES), place.step(place.row, -e)), b_rs.at[i])
    vec[...] = vec_in[0] + vec_in[1]
    for layer in range(2):
        for row in range(side):
            at = pl.ds(row * head, head)
            for t in range(3):
                i = layer * 3 + t
                bq[layer:layer + 1, row * triple + t * head:row * triple + (t + 1) * head] = bias_in[0, i:i + 1, at] + bias_in[1, i:i + 1, at]
            tiles = wide // head
            for t in range(tiles):
                i = 6 + layer * tiles + t
                bu[layer:layer + 1, row * wide + t * head:row * wide + (t + 1) * head] = bias_in[0, i:i + 1, at] + bias_in[1, i:i + 1, at]

    go.forward()
    x_ring.forward()
    exchange(1, 0, wq1)
    exchange(1, 1, wu1)
    gq.forward()
    gu.forward()
    gd.start()

    tile = min(32, half)

    def norm(src, doc, layer, which):
        gain, shift = vec[layer * 4 + which:layer * 4 + which + 1, :], vec[layer * 4 + which + 1:layer * 4 + which + 2, :]

        @pl.loop(0, seq, step=tile)
        def _(r):
            rows = src[doc, pl.ds(r, tile), :].astype(f32)
            centered = rows - jnp.mean(rows, axis=-1, keepdims=True)
            var = jnp.mean(centered * centered, axis=-1, keepdims=True)
            a_buf[pl.ds(r, tile), :] = (centered * lax.rsqrt(var + LN_EPS) * gain + shift).astype(bf)

    def attend(doc, layer):
        chip = place.row * side + doc
        lens = vec[12:13, pl.ds(pl.multiple_of(chip * head, head), head)]
        lane = lax.broadcasted_iota(jnp.int32, (1, head), 1)
        length = jnp.sum(jnp.where(lane == place.core * (head // CORES), lens, 0.0), axis=1, keepdims=True)
        query = lax.broadcasted_iota(jnp.int32, (seq, seq), 0)
        key = lax.broadcasted_iota(jnp.int32, (seq, seq), 1)
        visible = (key <= query) & (key.astype(f32) < length)
        pair = 2 * triple

        def turn(u):
            u = u.astype(f32)
            shift = head // 8
            return (u * rot_ref[0] + pltpu.roll(u, head - shift, 1) * rot_ref[1] + pltpu.roll(u, shift, 1) * rot_ref[2]).astype(bf)

        @pl.loop(0, per // 2)
        def _(p):
            at = pl.ds(pl.multiple_of(p * pair, pair), pair)
            w = wq[:, :, :, :, at].reshape(d_model, pair)
            qkv = (jnp.dot(a_buf[...], w, preferred_element_type=f32) + bq[layer:layer + 1, at]).astype(bf)
            for h in range(2):
                q, k, v = (qkv[:, h * triple + j * head:h * triple + (j + 1) * head] for j in range(3))
                scores = lax.dot_general(turn(q), turn(k), (((1,), (1,)), ((), ())), preferred_element_type=f32) * (head ** -0.5)
                scores = jnp.where(visible, scores, -1e30)
                probs = jnp.exp(scores - jnp.max(scores, axis=-1, keepdims=True))
                probs = (probs / jnp.sum(probs, axis=-1, keepdims=True)).astype(bf)
                to = pl.ds(pl.multiple_of((p * 2 + h) * head, head), head)
                ctx[doc, :, to] = jnp.dot(probs, v, preferred_element_type=f32).astype(bf)

    def up(doc, layer):
        step = ff // 4

        @pl.loop(0, 4)
        def _(n):
            at = pl.ds(pl.multiple_of(n * step, step), step)
            u = jnp.dot(a_buf[...], wu[:, :, :, :, at].reshape(d_model, step), preferred_element_type=f32) + bu[layer:layer + 1, at]
            act[doc, :, at] = (0.5 * u * (1.0 + lax.erf(u * (0.5 ** 0.5)))).astype(bf)

    def down(doc):
        step = d_model // 4

        @pl.loop(0, 4)
        def _(n):
            at = pl.ds(pl.multiple_of(n * step, step), step)
            tot = jnp.dot(ctx[doc], wo[:, :, :, at].reshape(per * head, step), preferred_element_type=f32)
            part[doc, :, at] = tot + jnp.dot(act[doc], wd[:, :, :, at].reshape(ff, step), preferred_element_type=f32)

    top, low = pl.ds(0, half), pl.ds(half, half)

    def send_far(layer):
        send(part.at[far, top], hop_a, r_ss.at[layer, 0], r_rs.at[layer, 0], left)
        send(part.at[far, low], hop_b, r_ss.at[layer, 1], r_rs.at[layer, 1], right)

    def send_prv(layer):
        send(part.at[prv, low], fin.at[0], r_ss.at[layer, 2], r_rs.at[layer, 2], left)

    def send_nxt(layer):
        send(part.at[nxt, top], fin.at[1], r_ss.at[layer, 3], r_rs.at[layer, 3], right)

    def pass_on(layer, i, hop, doc, first, dev):
        settle(hop, r_rs.at[layer, i])

        @pl.loop(0, half, step=tile)
        def _(r):
            hop[pl.ds(r, tile), :] = hop[pl.ds(r, tile), :] + part[doc, pl.ds(first + r, tile), :]

        send(hop, fin.at[2 + i], r_ss.at[layer, 4 + i], r_rs.at[layer, 4 + i], dev)

    def total(layer, src, first, f_one, f_two, store):
        @pl.loop(0, half, step=tile)
        def _(r):
            here, at = pl.ds(r, tile), pl.ds(first + r, tile)
            tot = part[place.col, at, :] + fin[f_one, here, :] + fin[f_two, here, :]
            bias = vec[8 + layer:9 + layer, :] + vec[10 + layer:11 + layer, :]
            store(at, (src[place.col, at, :].astype(f32) + (tot + bias)).astype(bf))

    def owner_sums(layer, src, store, done):
        for i in range(2, 6):
            settle(fin.at[0], r_rs.at[layer, i])
        total(layer, src, 0, 1, 2, store)
        total(layer, src, half, 0, 3, store)
        done()

    def sums_sent(layer):
        for i in range(6):
            settle(hop_a, r_ss.at[layer, i])

    settle(xg.at[place.col], loc.at[0])
    x_ring.rest()
    x_ring.last()
    gq.finish()

    @pl.loop(0, side)
    def _(doc):
        norm(xg, doc, 0, 0)
        attend(doc, 0)

    gu.finish()

    @pl.loop(0, side)
    def _(doc):
        norm(xg, doc, 0, 2)
        up(doc, 0)

        @pl.when(doc == 1)
        def _():
            gd.forward()

    go.finish()
    exchanged(1, 0, wq1)
    exchanged(1, 1, wu1)
    gq1.start()
    gu1.start()
    go1.start()
    gd1.start()
    settle(wo.at[place.row, place.core], loc.at[1])
    settle(wd.at[place.row, place.core], loc.at[2])
    gd.finish()

    @pl.loop(0, side)
    def _(i):
        doc = lax.rem(place.col + jnp.where(i == 0, 2, jnp.where(i == 1, 1, jnp.where(i == 2, side - 1, 0))), side)
        down(doc)

        @pl.when(i == 0)
        def _():
            send_far(0)

        @pl.when(i == 1)
        def _():
            send_nxt(0)

        @pl.when(i == 2)
        def _():
            send_prv(0)

    for g in gathers[0]:
        g.drain()
    gq1.forward()
    pass_on(0, 0, hop_a, prv, 0, left)
    pass_on(0, 1, hop_b, nxt, half, right)
    gu1.forward()
    go1.forward()

    def keep(at, rows):
        xg1[place.col, at, :] = rows

    owner_sums(0, xg, keep, x1_ring.start)
    gd1.forward()
    gq1.finish()
    load = [pltpu.make_async_copy(src, dst, loc1.at[i]) for i, (src, dst) in enumerate(((wq1, wq), (wu1, wu), (wo1, wo), (wd1, wd)))]
    load[0].start()
    sums_sent(0)
    load[0].wait()

    @pl.loop(0, side)
    def _(i):
        doc = lax.rem(place.col + jnp.where(i == 0, 0, jnp.where(i == 1, 1, jnp.where(i == 2, side - 1, 2))), side)

        @pl.when(i == 1)
        def _():
            x1_ring.rest()

        @pl.when(i == 3)
        def _():
            x1_ring.last()

        norm(xg1, doc, 1, 0)
        attend(doc, 1)

        @pl.when(i == 0)
        def _():
            x1_ring.forward()
            gu1.finish()
            pltpu.make_async_copy(wu1, wu, loc1.at[1]).start()
            go1.finish()
            settle(wo1.at[place.row, place.core], loc.at[3])
            pltpu.make_async_copy(wo1, wo, loc1.at[2]).start()
            settle(wu, loc1.at[1])

        norm(xg1, doc, 1, 2)
        up(doc, 1)

        @pl.when(i == 0)
        def _():
            settle(wd1.at[place.row, place.core], loc.at[4])
            gd1.finish()
            pltpu.make_async_copy(wd1, wd, loc1.at[3]).start()
            settle(wo, loc1.at[2])
            settle(wd, loc1.at[3])

        down(doc)

        @pl.when(i == 1)
        def _():
            send_nxt(1)

        @pl.when(i == 2)
        def _():
            send_prv(1)

        @pl.when(i == 3)
        def _():
            send_far(1)

    pass_on(1, 0, hop_a, prv, 0, left)
    pass_on(1, 1, hop_b, nxt, half, right)

    def give_out(at, rows):
        out_ref[at, :] = rows

    owner_sums(1, xg1, give_out, lambda: None)
    sums_sent(1)
    for g in gathers[1]:
        g.drain()
    x_ring.drain()
    x1_ring.drain()
    for d in range(count - 1):
        settle(vec_ref, v_ss.at[d])
    for i in range(len(column)):
        settle(bias_ref, b_ss.at[i])
    for layer in range(2):
        for kind, buf in enumerate((wq, wu)):
            for d in range(1, side):
                settle(buf.at[0, 0, 0], a_ss.at[layer, kind, d])


VM = pl.BlockSpec(memory_space=pltpu.VMEM)
ANY = pl.BlockSpec(memory_space=pl.ANY)
DMA = pltpu.SemaphoreType.DMA


def solution(mesh):
    row_spec = P(('dp', 'fsdp'), None, None)
    in_specs = (row_spec, P(('dp', 'fsdp')), P(None, None, 'fsdp'), P(None, 'fsdp', None, None), P(None, 'fsdp'), P(None, 'fsdp', None), P(None, 'fsdp'), P(None, 'fsdp', None), P(None, 'fsdp'), P(None, 'fsdp', None), P(None, 'fsdp'))
    count = mesh.shape['fsdp']
    side = math.isqrt(count // CORES)

    def local_step(hidden_loc, lens_loc, ln_par, w_qkv, b_qkv, w_out, b_out, w_up, b_up, w_down, b_down):
        layers = ln_par.shape[0]
        _, seq_len, d_model = hidden_loc.shape
        d_rows, heads, triple = w_qkv.shape[1:]
        head_dim = triple // 3
        per = heads // side
        ff_rows = w_down.shape[1]
        ff = ff_rows * CORES * side
        bf, f32 = jnp.bfloat16, jnp.float32
        core = lax.axis_index('fsdp') % CORES

        def placed(vals):
            zero = jnp.zeros_like(vals)
            return jnp.where(core == 0, jnp.concatenate([vals, zero], axis=-1), jnp.concatenate([zero, vals], axis=-1))

        lens_row = jnp.broadcast_to(lens_loc.astype(f32)[:, None], (1, d_rows))
        vec = jnp.concatenate([ln_par.reshape(-1, d_rows), b_out.astype(f32), b_down.astype(f32), lens_row, jnp.zeros((3, d_rows), f32)], axis=0)
        vec = placed(vec)
        bias = jnp.concatenate([placed(b_qkv.astype(f32)).reshape(-1, head_dim), placed(b_up.astype(f32)).reshape(-1, head_dim)], axis=0)
        bias = jnp.pad(bias, ((0, -bias.shape[0] % 16), (0, 0)))
        wq = w_qkv.reshape(layers, d_rows, per, side, triple).transpose(0, 3, 1, 2, 4).reshape(layers, side, d_rows, per * triple)

        half = seq_len // 2
        wq_s, wu_s = (side, side, CORES, d_rows, per * triple), (side, side, CORES, d_rows, ff)
        wo_s, wd_s = (side, CORES) + w_out.shape[1:], (side, CORES) + w_down.shape[1:]
        outs = pl.pallas_call(
            functools.partial(both_layers, side),
            out_shape=(jax.ShapeDtypeStruct((seq_len, d_model), bf), *(jax.ShapeDtypeStruct(s, bf) for s in (wq_s, wu_s, wo_s, wd_s))),
            in_specs=[ANY, VM, VM, VM, ANY, ANY, ANY, ANY],
            out_specs=(VM, ANY, ANY, ANY, ANY),
            scratch_shapes=[
                *(pltpu.VMEM(s, bf) for s in (wq_s, wu_s, wo_s, wd_s)),
                pltpu.VMEM((side, seq_len, d_model), bf),
                pltpu.VMEM((side, seq_len, d_model), bf),
                pltpu.VMEM((seq_len, d_model), bf),
                pltpu.VMEM((side, seq_len, ff), bf),
                pltpu.VMEM((side, seq_len, per * head_dim), bf),
                pltpu.VMEM((side, seq_len, d_model), f32),
                pltpu.VMEM((half, d_model), f32),
                pltpu.VMEM((half, d_model), f32),
                pltpu.VMEM((4, half, d_model), f32),
                pltpu.VMEM((CORES, 16, d_model), f32),
                pltpu.VMEM((CORES, bias.shape[0], side * head_dim), f32),
                pltpu.VMEM((16, d_model), f32),
                pltpu.VMEM((layers, per * triple), f32),
                pltpu.VMEM((layers, ff), f32),
                DMA((count - 1,)), DMA((count - 1,)), DMA((side * CORES - 1,)), DMA((side * CORES - 1,)),
                DMA((2, 6)), DMA((2, 6)), DMA((2, 2, side)), DMA((2, 2, side)),
                DMA((2, 4, 6)), DMA((2, 4, 6)), DMA((2, 4, 8)), DMA((2, 4, 8)),
                DMA((2, 6)), DMA((2, 6)), DMA((5,)), DMA((4,)),
            ],
            compiler_params=pltpu.CompilerParams(collective_id=0, has_side_effects=True, vmem_limit_bytes=67043328),
        )(hidden_loc[0], vec, bias, rotary_factors(seq_len, head_dim), wq, w_up, w_out, w_down)
        return outs[0][None]

    return jax.shard_map(local_step, mesh=mesh, in_specs=in_specs, out_specs=row_spec, check_vma=False)
```

time: 763 us -> 357 us (0.47)
  Pallas kernels: 0 us -> 344 us
  waiting for transfers between devices: 226 us -> 0 us
  blocking collectives: 182 us -> 0 us
  local copies, waits for them, and re-layouts: 172 us -> 8.76 us
  matrix products: 141 us -> 0 us
  other arithmetic: 18.9 us -> 2.13 us
  between operations: 14.9 us -> 0.69 us
    pallas_call x0 -> x1, Pallas kernels: none -> 344 us  [local_step(): pl.pallas_call(functools.partial(both_layers, side), out_shape=(jax.Shape...]
    all_gather x8 -> x0, waiting for transfers between devices: 223 us -> none  [gather_full(): return lax.all_gather(piece, 'fsdp', axis=axis_idx, tiled=True)]
    dot_general x12 -> x0, matrix products: 141 us -> none  [the longest x2 63.7 us: layer_forward(): jnp.dot(mlp_in, w_up_full, preferred_element_type=jnp.float32)]
    all_gather x4 -> x0, blocking collectives: 130 us -> none  [gather_full(): return lax.all_gather(piece, 'fsdp', axis=axis_idx, tiled=True)]
    slice x15 -> x0, local copies, waits for them, and re-layouts: 99.4 us -> none  [the longest x2 86.5 us: layer_forward(): mlp_in = layer_norm(x_rows, ln_full[2], ln_full[3])]
    unnamed x83 -> x1, local copies, waits for them, and re-layouts: 68.8 us -> 2.3 us
    unnamed x1 -> x0, blocking collectives: 52.1 us -> none
  transfers between devices with their start and end apart: 8 -> 0, of which waited for: 3 -> 0; matrix products, arithmetic and copies ran while one was open for 41% -> 0% of each run, Pallas kernels for 0% -> 0%
where the time goes in v1:
time: 357 us; the launch traced here: 356 us
  Pallas kernels  344 us (96%)
  local copies, waits for them, and re-layouts  8.76 us (2%)
    pallas_call x1, Pallas kernels, local_step(): pl.pallas_call(functools.partial(both_layers, side), out_shape=(jax.Shape...  344 us

profile of v1, /device:TPU:97, one launch (start us, length us, event | category | flops | bytes accessed | tf_op | source)
XLA Modules:
  0.0 355.8 jit_solution(14720415945051370343)
XLA Ops:
  0.7 0.7 convert_element_type.20
  1.3 0.1 pad_select_fusion.2
  1.4 0.7 convert_element_type.21
  2.1 1.4 concatenate.24
  3.5 0.7 select_maximum_fusion
  4.2 2.9 reshape.21
  7.1 0.6 copy.15
  7.7 1.5 reshape.22.wq_ref
  9.3 344.3 %shard_map.118 = (bf16[256,2048]{1,0:T(8,128)(2,1)}, bf16[4,4,2,64,1536]{4,3,2,1,0:T(8,128)(2,1)}, bf16[4,4,2,64,2048]{4,3,2,1,0:T(8,128)(2,1)}, bf16[4,2,64,204...) custom-call(bf16[256,2048]{1,0:T(8,128)(2,1)} %bitcast.11, f32[16,128]{1,0:T(8,128)} %get-tuple-element.8.vec_ref, ...), custom_call_target="tpu_custom_call" | custom-call | tf_op jit(solution)/shard_map/pallas_call | solution.py:529
  353.5 2.3 copy.18
  (5 shorter events, 0.0 us)

commit v2 on v1

--- a/solution.py
+++ b/solution.py
@@ -138,12 +138,13 @@
 def weight_gathers(place, bufs, wo_own, wd_own, sems):
     wq, wu, wo, wd = bufs
     cols = wq.shape[1] // 2
-    o_rows, d_rows = wo.shape[2] // 2, wd.shape[2] // 2
+    o_rows, d_rows, d_cols = wo.shape[2] // 2, wd.shape[3] // 2, wd.shape[4]
     specs = (
         (lambda row, half, core: wq.at[row, pl.ds(half * cols, cols), core], None),
         (lambda row, half, core: wu.at[row, pl.ds(half * cols, cols), core], None),
         (lambda row, half, core: wo.at[row, core, pl.ds(half * o_rows, o_rows)], lambda half: wo_own.at[pl.ds(half * o_rows, o_rows)]),
-        (lambda row, half, core: wd.at[row, core, pl.ds(half * d_rows, d_rows)], lambda half: wd_own.at[pl.ds(half * d_rows, d_rows)]),
+        *((lambda row, half, core, h=h: wd.at[h, row, core, pl.ds(half * d_rows, d_rows)],
+           lambda half, h=h: wd_own.at[pl.ds(half * d_rows, d_rows), pl.ds(h * d_cols, d_cols)]) for h in range(2)),
     )
     return [Gather(place, blk, own, *(s.at[t] for s in sems)) for t, (blk, own) in enumerate(specs)]
 
@@ -195,8 +196,9 @@
         weight_gathers(place, (wq, wu, wo, wd), wo_ref.at[0], wd_ref.at[0], [s.at[0] for s in (w_ss, w_rs, c_ss, c_rs)]),
         weight_gathers(place, (wq1, wu1, wo1, wd1), wo_ref.at[1], wd_ref.at[1], [s.at[1] for s in (w_ss, w_rs, c_ss, c_rs)]),
     ]
-    gq, gu, go, gd = gathers[0]
-    gq1, gu1, go1, gd1 = gathers[1]
+    gq, gu, go, *gd = gathers[0]
+    gq1, gu1, go1, *gd1 = gathers[1]
+    d_cols = wd.shape[4]
     rows_of = lambda ref, col, h: ref.at[col, pl.ds(h * half, half)]
     x_ring = Ring(place, place.col, right, left, lambda col, h: rows_of(xg, col, h), lambda h: x_ref.at[pl.ds(h * half, half)], x_ss.at[0], x_rs.at[0])
     x1_ring = Ring(place, place.col, right, left, lambda col, h: rows_of(xg1, col, h), lambda h: rows_of(xg1, place.col, h), x_ss.at[1], x_rs.at[1])
@@ -212,9 +214,10 @@
         send(bias_ref, bias_at(place.core, place.row), b_ss.at[i], b_rs.at[i], dev)
     exchange(0, 1, wu)
     go.start()
+    gd[1].start()
     x_ring.start()
-    own = [(x_ref, xg.at[place.col]), (wo_ref.at[0], wo.at[place.row, place.core]), (wd_ref.at[0], wd.at[place.row, place.core]),
-           (wo_ref.at[1], wo1.at[place.row, place.core]), (wd_ref.at[1], wd1.at[place.row, place.core])]
+    own = [(x_ref, xg.at[place.col]), (wo_ref.at[0], wo.at[place.row, place.core]), (wo_ref.at[1], wo1.at[place.row, place.core])]
+    own += [(wd_ref.at[layer, :, pl.ds(h * d_cols, d_cols)], buf.at[h, place.row, place.core]) for layer, buf in enumerate((wd, wd1)) for h in range(2)]
     for i, (src, dst) in enumerate(own):
         pltpu.make_async_copy(src, dst, loc.at[i]).start()
 
@@ -249,7 +252,7 @@
     exchange(1, 1, wu1)
     gq.forward()
     gu.forward()
-    gd.start()
+    gd[0].start()
 
     tile = min(32, half)
 
@@ -301,54 +304,55 @@
             u = jnp.dot(a_buf[...], wu[:, :, :, :, at].reshape(d_model, step), preferred_element_type=f32) + bu[layer:layer + 1, at]
             act[doc, :, at] = (0.5 * u * (1.0 + lax.erf(u * (0.5 ** 0.5)))).astype(bf)
 
-    def down(doc):
-        step = d_model // 4
-
-        @pl.loop(0, 4)
+    def down(doc, h):
+        step = d_cols // 2
+
+        @pl.loop(0, 2)
         def _(n):
             at = pl.ds(pl.multiple_of(n * step, step), step)
-            tot = jnp.dot(ctx[doc], wo[:, :, :, at].reshape(per * head, step), preferred_element_type=f32)
-            part[doc, :, at] = tot + jnp.dot(act[doc], wd[:, :, :, at].reshape(ff, step), preferred_element_type=f32)
+            wide_at = pl.ds(pl.multiple_of(h * d_cols + n * step, step), step)
+            tot = jnp.dot(ctx[doc], wo[:, :, :, wide_at].reshape(per * head, step), preferred_element_type=f32)
+            part[doc, h, :, at] = tot + jnp.dot(act[doc], wd[h, :, :, :, at].reshape(ff, step), preferred_element_type=f32)
 
     top, low = pl.ds(0, half), pl.ds(half, half)
 
-    def send_far(layer):
-        send(part.at[far, top], hop_a, r_ss.at[layer, 0], r_rs.at[layer, 0], left)
-        send(part.at[far, low], hop_b, r_ss.at[layer, 1], r_rs.at[layer, 1], right)
-
-    def send_prv(layer):
-        send(part.at[prv, low], fin.at[0], r_ss.at[layer, 2], r_rs.at[layer, 2], left)
-
-    def send_nxt(layer):
-        send(part.at[nxt, top], fin.at[1], r_ss.at[layer, 3], r_rs.at[layer, 3], right)
-
-    def pass_on(layer, i, hop, doc, first, dev):
-        settle(hop, r_rs.at[layer, i])
-
-        @pl.loop(0, half, step=tile)
-        def _(r):
-            hop[pl.ds(r, tile), :] = hop[pl.ds(r, tile), :] + part[doc, pl.ds(first + r, tile), :]
-
-        send(hop, fin.at[2 + i], r_ss.at[layer, 4 + i], r_rs.at[layer, 4 + i], dev)
-
-    def total(layer, src, first, f_one, f_two, store):
-        @pl.loop(0, half, step=tile)
-        def _(r):
-            here, at = pl.ds(r, tile), pl.ds(first + r, tile)
-            tot = part[place.col, at, :] + fin[f_one, here, :] + fin[f_two, here, :]
-            bias = vec[8 + layer:9 + layer, :] + vec[10 + layer:11 + layer, :]
-            store(at, (src[place.col, at, :].astype(f32) + (tot + bias)).astype(bf))
-
-    def owner_sums(layer, src, store, done):
-        for i in range(2, 6):
-            settle(fin.at[0], r_rs.at[layer, i])
-        total(layer, src, 0, 1, 2, store)
-        total(layer, src, half, 0, 3, store)
-        done()
+    def send_far(layer, h):
+        send(part.at[far, h, top], hop_a.at[h], r_ss.at[layer, h, 0], r_rs.at[layer, h, 0], left)
+        send(part.at[far, h, low], hop_b.at[h], r_ss.at[layer, h, 1], r_rs.at[layer, h, 1], right)
+
+    def send_prv(layer, h):
+        send(part.at[prv, h, low], fin.at[0, h], r_ss.at[layer, h, 2], r_rs.at[layer, h, 2], left)
+
+    def send_nxt(layer, h):
+        send(part.at[nxt, h, top], fin.at[1, h], r_ss.at[layer, h, 3], r_rs.at[layer, h, 3], right)
+
+    def pass_on(layer, h):
+        for i, hop, doc, first, dev in ((0, hop_a, prv, 0, left), (1, hop_b, nxt, half, right)):
+            settle(hop.at[h], r_rs.at[layer, h, i])
+
+            @pl.loop(0, half, step=tile)
+            def _(r, hop=hop, doc=doc, first=first):
+                hop[h, pl.ds(r, tile), :] = hop[h, pl.ds(r, tile), :] + part[doc, h, pl.ds(first + r, tile), :]
+
+            send(hop.at[h], fin.at[2 + i, h], r_ss.at[layer, h, 4 + i], r_rs.at[layer, h, 4 + i], dev)
+
+    def owner_sums(layer, src, store):
+        for h in range(2):
+            cols = slice(h * d_cols, (h + 1) * d_cols)
+            for i in range(2, 6):
+                settle(fin.at[i - 2, h], r_rs.at[layer, h, i])
+            for first, f_one, f_two in ((0, 1, 2), (half, 0, 3)):
+                @pl.loop(0, half, step=tile)
+                def _(r, first=first, f_one=f_one, f_two=f_two):
+                    here, at = pl.ds(r, tile), pl.ds(first + r, tile)
+                    tot = part[place.col, h, at, :] + fin[f_one, h, here, :] + fin[f_two, h, here, :]
+                    bias = vec[8 + layer:9 + layer, cols] + vec[10 + layer:11 + layer, cols]
+                    store(at, cols, (src[place.col, at, cols].astype(f32) + (tot + bias)).astype(bf))
 
     def sums_sent(layer):
-        for i in range(6):
-            settle(hop_a, r_ss.at[layer, i])
+        for h in range(2):
+            for i in range(6):
+                settle(hop_a.at[h], r_ss.at[layer, h, i])
 
     settle(xg.at[place.col], loc.at[0])
     x_ring.rest()
@@ -369,54 +373,60 @@
 
         @pl.when(doc == 1)
         def _():
-            gd.forward()
-
+            gd[0].forward()
+
+    gd[1].forward()
     go.finish()
+    settle(wo.at[place.row, place.core], loc.at[1])
     exchanged(1, 0, wq1)
     exchanged(1, 1, wu1)
     gq1.start()
     gu1.start()
+
+    for h in range(2):
+        settle(wd.at[h, place.row, place.core], loc.at[3 + h])
+        gd[h].finish()
+
+        @pl.loop(0, side)
+        def _(i, h=h):
+            doc = lax.rem(place.col + jnp.where(i == 0, 2, jnp.where(i == 1, 1, jnp.where(i == 2, side - 1, 0))), side)
+            down(doc, h)
+
+            @pl.when(i == 0)
+            def _():
+                send_far(0, h)
+
+            @pl.when(i == 1)
+            def _():
+                send_nxt(0, h)
+
+            @pl.when(i == 2)
+            def _():
+                send_prv(0, h)
+
+    gq1.forward()
+    pass_on(0, 0)
+    pass_on(0, 1)
+    gu1.forward()
     go1.start()
-    gd1.start()
-    settle(wo.at[place.row, place.core], loc.at[1])
-    settle(wd.at[place.row, place.core], loc.at[2])
-    gd.finish()
-
-    @pl.loop(0, side)
-    def _(i):
-        doc = lax.rem(place.col + jnp.where(i == 0, 2, jnp.where(i == 1, 1, jnp.where(i == 2, side - 1, 0))), side)
-        down(doc)
-
-        @pl.when(i == 0)
-        def _():
-            send_far(0)
-
-        @pl.when(i == 1)
-        def _():
-            send_nxt(0)
-
-        @pl.when(i == 2)
-        def _():
-            send_prv(0)
-
+    gd1[0].start()
+    gd1[1].start()
     for g in gathers[0]:
         g.drain()
-    gq1.forward()
-    pass_on(0, 0, hop_a, prv, 0, left)
-    pass_on(0, 1, hop_b, nxt, half, right)
-    gu1.forward()
+    gq1.finish()
+    pltpu.make_async_copy(wq1, wq, loc1.at[0]).start()
+    gu1.finish()
+    pltpu.make_async_copy(wu1, wu, loc1.at[1]).start()
+
+    def keep(at, cols, rows):
+        xg1[place.col, at, cols] = rows
+
+    owner_sums(0, xg, keep)
+    x1_ring.start()
     go1.forward()
-
-    def keep(at, rows):
-        xg1[place.col, at, :] = rows
-
-    owner_sums(0, xg, keep, x1_ring.start)
-    gd1.forward()
-    gq1.finish()
-    load = [pltpu.make_async_copy(src, dst, loc1.at[i]) for i, (src, dst) in enumerate(((wq1, wq), (wu1, wu), (wo1, wo), (wd1, wd)))]
-    load[0].start()
     sums_sent(0)
-    load[0].wait()
+    settle(wq, loc1.at[0])
+    settle(wu, loc1.at[1])
 
     @pl.loop(0, side)
     def _(i):
@@ -426,55 +436,62 @@
         def _():
             x1_ring.rest()
 
+        @pl.when(i == 2)
+        def _():
+            settle(wo1.at[place.row, place.core], loc.at[2])
+            go1.finish()
+            pltpu.make_async_copy(wo1, wo, loc1.at[2]).start()
+            settle(wd1.at[0, place.row, place.core], loc.at[5])
+            gd1[0].finish()
+            pltpu.make_async_copy(wd1.at[0], wd.at[0], loc1.at[3]).start()
+
         @pl.when(i == 3)
         def _():
             x1_ring.last()
 
         norm(xg1, doc, 1, 0)
         attend(doc, 1)
-
-        @pl.when(i == 0)
-        def _():
-            x1_ring.forward()
-            gu1.finish()
-            pltpu.make_async_copy(wu1, wu, loc1.at[1]).start()
-            go1.finish()
-            settle(wo1.at[place.row, place.core], loc.at[3])
-            pltpu.make_async_copy(wo1, wo, loc1.at[2]).start()
-            settle(wu, loc1.at[1])
-
         norm(xg1, doc, 1, 2)
         up(doc, 1)
 
         @pl.when(i == 0)
         def _():
-            settle(wd1.at[place.row, place.core], loc.at[4])
-            gd1.finish()
-            pltpu.make_async_copy(wd1, wd, loc1.at[3]).start()
+            x1_ring.forward()
+            gd1[0].forward()
+            gd1[1].forward()
+
+        @pl.when(i == 2)
+        def _():
+            settle(wd1.at[1, place.row, place.core], loc.at[6])
+            gd1[1].finish()
+            pltpu.make_async_copy(wd1.at[1], wd.at[1], loc1.at[4]).start()
             settle(wo, loc1.at[2])
-            settle(wd, loc1.at[3])
-
-        down(doc)
-
-        @pl.when(i == 1)
-        def _():
-            send_nxt(1)
-
-        @pl.when(i == 2)
-        def _():
-            send_prv(1)
+            settle(wd.at[0], loc1.at[3])
+            down(nxt, 0)
+            send_nxt(1, 0)
+            down(prv, 0)
+            send_prv(1, 0)
+            settle(wd.at[1], loc1.at[4])
+            down(nxt, 1)
+            send_nxt(1, 1)
+            down(prv, 1)
+            send_prv(1, 1)
 
         @pl.when(i == 3)
         def _():
-            send_far(1)
-
-    pass_on(1, 0, hop_a, prv, 0, left)
-    pass_on(1, 1, hop_b, nxt, half, right)
-
-    def give_out(at, rows):
-        out_ref[at, :] = rows
-
-    owner_sums(1, xg1, give_out, lambda: None)
+            for h in range(2):
+                down(far, h)
+                send_far(1, h)
+            for h in range(2):
+                down(place.col, h)
+
+    pass_on(1, 0)
+    pass_on(1, 1)
+
+    def give_out(at, cols, rows):
+        out_ref[at, cols] = rows
+
+    owner_sums(1, xg1, give_out)
     sums_sent(1)
     for g in gathers[1]:
         g.drain()
@@ -525,7 +542,7 @@
 
         half = seq_len // 2
         wq_s, wu_s = (side, side, CORES, d_rows, per * triple), (side, side, CORES, d_rows, ff)
-        wo_s, wd_s = (side, CORES) + w_out.shape[1:], (side, CORES) + w_down.shape[1:]
+        wo_s, wd_s = (side, CORES) + w_out.shape[1:], (2, side, CORES, ff_rows, d_model // 2)
         outs = pl.pallas_call(
             functools.partial(both_layers, side),
             out_shape=(jax.ShapeDtypeStruct((seq_len, d_model), bf), *(jax.ShapeDtypeStruct(s, bf) for s in (wq_s, wu_s, wo_s, wd_s))),
@@ -538,10 +555,10 @@
                 pltpu.VMEM((seq_len, d_model), bf),
                 pltpu.VMEM((side, seq_len, ff), bf),
                 pltpu.VMEM((side, seq_len, per * head_dim), bf),
-                pltpu.VMEM((side, seq_len, d_model), f32),
-                pltpu.VMEM((half, d_model), f32),
-                pltpu.VMEM((half, d_model), f32),
-                pltpu.VMEM((4, half, d_model), f32),
+                pltpu.VMEM((side, 2, seq_len, d_model // 2), f32),
+                pltpu.VMEM((2, half, d_model // 2), f32),
+                pltpu.VMEM((2, half, d_model // 2), f32),
+                pltpu.VMEM((4, 2, half, d_model // 2), f32),
                 pltpu.VMEM((CORES, 16, d_model), f32),
                 pltpu.VMEM((CORES, bias.shape[0], side * head_dim), f32),
                 pltpu.VMEM((16, d_model), f32),
@@ -549,8 +566,8 @@
                 pltpu.VMEM((layers, ff), f32),
                 DMA((count - 1,)), DMA((count - 1,)), DMA((side * CORES - 1,)), DMA((side * CORES - 1,)),
                 DMA((2, 6)), DMA((2, 6)), DMA((2, 2, side)), DMA((2, 2, side)),
-                DMA((2, 4, 6)), DMA((2, 4, 6)), DMA((2, 4, 8)), DMA((2, 4, 8)),
-                DMA((2, 6)), DMA((2, 6)), DMA((5,)), DMA((4,)),
+                DMA((2, 5, 6)), DMA((2, 5, 6)), DMA((2, 5, 8)), DMA((2, 5, 8)),
+                DMA((2, 2, 6)), DMA((2, 2, 6)), DMA((7,)), DMA((5,)),
             ],
             compiler_params=pltpu.CompilerParams(collective_id=0, has_side_effects=True, vmem_limit_bytes=67043328),
         )(hidden_loc[0], vec, bias, rotary_factors(seq_len, head_dim), wq, w_up, w_out, w_down)

time: 357 us -> 351 us (0.983)
  Pallas kernels: 344 us -> 339 us
    pallas_call x1, Pallas kernels: 344 us -> 339 us  [local_step(): pl.pallas_call(functools.partial(both_layers, side), out_shape=(jax.Shape...]
where the time goes in v2:
time: 351 us
  Pallas kernels  339 us (97%)
  local copies, waits for them, and re-layouts  8.76 us (2%)
    pallas_call x1, Pallas kernels, local_step(): pl.pallas_call(functools.partial(both_layers, side), out_shape=(jax.Shape...  339 us

profile of v2, /device:TPU:97, one launch (start us, length us, event | category | flops | bytes accessed | tf_op | source)
XLA Modules:
  0.0 350.7 jit_solution(4713424153378386003)
XLA Ops:
  0.7 0.7 convert_element_type.20
  1.3 0.1 pad_select_fusion.2
  1.4 0.7 convert_element_type.21
  2.1 1.4 concatenate.24
  3.5 0.7 select_maximum_fusion
  4.2 2.9 reshape.21
  7.1 0.6 copy.15
  7.7 1.5 reshape.22.wq_ref
  9.3 339.2 %shard_map.118 = (bf16[256,2048]{1,0:T(8,128)(2,1)}, bf16[4,4,2,64,1536]{4,3,2,1,0:T(8,128)(2,1)}, bf16[4,4,2,64,2048]{4,3,2,1,0:T(8,128)(2,1)}, bf16[4,2,64,204...) custom-call(bf16[256,2048]{1,0:T(8,128)(2,1)} %bitcast.11, f32[16,128]{1,0:T(8,128)} %get-tuple-element.8.vec_ref, ...), custom_call_target="tpu_custom_call" | custom-call | tf_op jit(solution)/shard_map/pallas_call | solution.py:546
  348.4 2.3 copy.18
  (5 shorter events, 0.0 us)

commit v3 on v2

--- a/solution.py
+++ b/solution.py
@@ -151,7 +151,7 @@
 
 def both_layers(side, x_ref, vec_ref, bias_ref, rot_ref, wq_ref, wu_ref, wo_ref, wd_ref,
                 out_ref, wq1, wu1, wo1, wd1,
-                wq, wu, wo, wd, xg, xg1, a_buf, act, ctx, part, hop_a, hop_b, fin, vec_in, bias_in, vec, bq, bu,
+                wq, wu, wo, wd, xg, xg1, a_buf, m_buf, act, ctx, part, hop_a, hop_b, fin, vec_in, bias_in, vec, bq, bu,
                 v_ss, v_rs, b_ss, b_rs, x_ss, x_rs, a_ss, a_rs, w_ss, w_rs, c_ss, c_rs, r_ss, r_rs, loc, loc1):
     f32, bf = jnp.float32, jnp.bfloat16
     place = Place(side)
@@ -227,6 +227,7 @@
     exchanged(0, 0, wq)
     gq.start()
     exchanged(0, 1, wu)
+    gq.forward()
     gu.start()
 
     for d in range(1, count):
@@ -246,25 +247,25 @@
                 i = 6 + layer * tiles + t
                 bu[layer:layer + 1, row * wide + t * head:row * wide + (t + 1) * head] = bias_in[0, i:i + 1, at] + bias_in[1, i:i + 1, at]
 
-    go.forward()
     x_ring.forward()
     exchange(1, 0, wq1)
     exchange(1, 1, wu1)
-    gq.forward()
-    gu.forward()
-    gd[0].start()
+    go.forward()
 
     tile = min(32, half)
 
-    def norm(src, doc, layer, which):
-        gain, shift = vec[layer * 4 + which:layer * 4 + which + 1, :], vec[layer * 4 + which + 1:layer * 4 + which + 2, :]
+    def norm(src, doc, layer):
+        par = [vec[layer * 4 + i:layer * 4 + i + 1, :] for i in range(4)]
 
         @pl.loop(0, seq, step=tile)
         def _(r):
-            rows = src[doc, pl.ds(r, tile), :].astype(f32)
+            at = pl.ds(r, tile)
+            rows = src[doc, at, :].astype(f32)
             centered = rows - jnp.mean(rows, axis=-1, keepdims=True)
             var = jnp.mean(centered * centered, axis=-1, keepdims=True)
-            a_buf[pl.ds(r, tile), :] = (centered * lax.rsqrt(var + LN_EPS) * gain + shift).astype(bf)
+            normed = centered * lax.rsqrt(var + LN_EPS)
+            a_buf[at, :] = (normed * par[0] + par[1]).astype(bf)
+            m_buf[doc, at, :] = (normed * par[2] + par[3]).astype(bf)
 
     def attend(doc, layer):
         chip = place.row * side + doc
@@ -296,20 +297,19 @@
                 ctx[doc, :, to] = jnp.dot(probs, v, preferred_element_type=f32).astype(bf)
 
     def up(doc, layer):
-        step = ff // 4
-
-        @pl.loop(0, 4)
-        def _(n):
-            at = pl.ds(pl.multiple_of(n * step, step), step)
-            u = jnp.dot(a_buf[...], wu[:, :, :, :, at].reshape(d_model, step), preferred_element_type=f32) + bu[layer:layer + 1, at]
-            act[doc, :, at] = (0.5 * u * (1.0 + lax.erf(u * (0.5 ** 0.5)))).astype(bf)
-
-    def down(doc, h):
-        step = d_cols // 2
+        step = ff // 8
 
         @pl.loop(0, 2)
         def _(n):
-            at = pl.ds(pl.multiple_of(n * step, step), step)
+            for j in range(4):
+                at = pl.ds(pl.multiple_of((n * 4 + j) * step, step), step)
+                u = jnp.dot(m_buf[doc], wu[:, :, :, :, at].reshape(d_model, step), preferred_element_type=f32) + bu[layer:layer + 1, at]
+                act[doc, :, at] = (0.5 * u * (1.0 + lax.erf(u * (0.5 ** 0.5)))).astype(bf)
+
+    def down(doc, h):
+        step = d_cols // 4
+        for n in range(4):
+            at = pl.ds(n * step, step)
             wide_at = pl.ds(pl.multiple_of(h * d_cols + n * step, step), step)
             tot = jnp.dot(ctx[doc], wo[:, :, :, wide_at].reshape(per * head, step), preferred_element_type=f32)
             part[doc, h, :, at] = tot + jnp.dot(act[doc], wd[h, :, :, :, at].reshape(ff, step), preferred_element_type=f32)
@@ -354,34 +354,52 @@
             for i in range(6):
                 settle(hop_a.at[h], r_ss.at[layer, h, i])
 
+    def nearest_first(i):
+        return lax.rem(place.col + jnp.where(i == 0, 0, jnp.where(i == 1, 1, jnp.where(i == 2, side - 1, 2))), side)
+
     settle(xg.at[place.col], loc.at[0])
-    x_ring.rest()
-    x_ring.last()
     gq.finish()
+
+    @pl.loop(0, side)
+    def _(i):
+        doc = nearest_first(i)
+
+        @pl.when(i == 1)
+        def _():
+            x_ring.rest()
+
+        @pl.when(i == 2)
+        def _():
+            gu.forward()
+            gd[0].start()
+
+        @pl.when(i == 3)
+        def _():
+            x_ring.last()
+
+        norm(xg, doc, 0)
+        attend(doc, 0)
+
+    gu.finish()
 
     @pl.loop(0, side)
     def _(doc):
-        norm(xg, doc, 0, 0)
-        attend(doc, 0)
-
-    gu.finish()
-
-    @pl.loop(0, side)
-    def _(doc):
-        norm(xg, doc, 0, 2)
         up(doc, 0)
 
+        @pl.when(doc == 0)
+        def _():
+            gd[0].forward()
+            gd[1].forward()
+
         @pl.when(doc == 1)
         def _():
-            gd[0].forward()
-
-    gd[1].forward()
+            exchanged(1, 0, wq1)
+            exchanged(1, 1, wu1)
+            gq1.start()
+            gu1.start()
+
     go.finish()
     settle(wo.at[place.row, place.core], loc.at[1])
-    exchanged(1, 0, wq1)
-    exchanged(1, 1, wu1)
-    gq1.start()
-    gu1.start()
 
     for h in range(2):
         settle(wd.at[h, place.row, place.core], loc.at[3 + h])
@@ -430,7 +448,7 @@
 
     @pl.loop(0, side)
     def _(i):
-        doc = lax.rem(place.col + jnp.where(i == 0, 0, jnp.where(i == 1, 1, jnp.where(i == 2, side - 1, 2))), side)
+        doc = nearest_first(i)
 
         @pl.when(i == 1)
         def _():
@@ -449,9 +467,8 @@
         def _():
             x1_ring.last()
 
-        norm(xg1, doc, 1, 0)
+        norm(xg1, doc, 1)
         attend(doc, 1)
-        norm(xg1, doc, 1, 2)
         up(doc, 1)
 
         @pl.when(i == 0)
@@ -553,6 +570,7 @@
                 pltpu.VMEM((side, seq_len, d_model), bf),
                 pltpu.VMEM((side, seq_len, d_model), bf),
                 pltpu.VMEM((seq_len, d_model), bf),
+                pltpu.VMEM((side, seq_len, d_model), bf),
                 pltpu.VMEM((side, seq_len, ff), bf),
                 pltpu.VMEM((side, seq_len, per * head_dim), bf),
                 pltpu.VMEM((side, 2, seq_len, d_model // 2), f32),

time: 351 us -> 322 us (0.917)
  Pallas kernels: 339 us -> 310 us
    pallas_call x1, Pallas kernels: 339 us -> 310 us  [local_step(): pl.pallas_call(functools.partial(both_layers, side), out_shape=(jax.Shape...]
where the time goes in v3:
time: 322 us
  Pallas kernels  310 us (96%)
  local copies, waits for them, and re-layouts  8.76 us (3%)
    pallas_call x1, Pallas kernels, local_step(): pl.pallas_call(functools.partial(both_layers, side), out_shape=(jax.Shape...  310 us

profile of v3, /device:TPU:97, one launch (start us, length us, event | category | flops | bytes accessed | tf_op | source)
XLA Modules:
  0.0 321.9 jit_solution(576428132556597834)
XLA Ops:
  0.7 0.7 convert_element_type.20
  1.3 0.1 pad_select_fusion.2
  1.4 0.7 convert_element_type.21
  2.1 1.4 concatenate.24
  3.5 0.7 select_maximum_fusion
  4.2 2.9 reshape.21
  7.1 0.6 copy.15
  7.7 1.5 reshape.22.wq_ref
  9.3 310.3 %shard_map.118 = (bf16[256,2048]{1,0:T(8,128)(2,1)}, bf16[4,4,2,64,1536]{4,3,2,1,0:T(8,128)(2,1)}, bf16[4,4,2,64,2048]{4,3,2,1,0:T(8,128)(2,1)}, bf16[4,2,64,204...) custom-call(bf16[256,2048]{1,0:T(8,128)(2,1)} %bitcast.11, f32[16,128]{1,0:T(8,128)} %get-tuple-element.8.vec_ref, ...), custom_call_target="tpu_custom_call" | custom-call | tf_op jit(solution)/shard_map/pallas_call | solution.py:563
  319.6 2.3 copy.18
  (5 shorter events, 0.0 us)

commit v4 on v3

--- a/solution.py
+++ b/solution.py
@@ -109,6 +109,8 @@
 
     def start(self):
         self.ring.start()
+
+    def own(self):
         self.give(0, 0, self.ring.own(0))
         self.give(0, 1, self.ring.own(1))
 
@@ -117,13 +119,17 @@
         self.give(1, 0)
         self.give(2, 1)
 
-    def finish(self):
+    def hand(self):
         self.ring.rest()
         self.give(1, 1)
         self.give(2, 0)
+
+    def tail(self):
         self.ring.last()
         self.give(3, 0)
         self.give(3, 1)
+
+    def take(self):
         for rel in range(4):
             for half in range(2):
                 settle(self.theirs(self.blocks[rel], half), self.cr.at[rel * 2 + half])
@@ -149,9 +155,9 @@
     return [Gather(place, blk, own, *(s.at[t] for s in sems)) for t, (blk, own) in enumerate(specs)]
 
 
-def both_layers(side, x_ref, vec_ref, bias_ref, rot_ref, wq_ref, wu_ref, wo_ref, wd_ref,
+def both_layers(side, x_ref, lens_ref, ln_ref, bq_ref, bo_ref, bu_ref, bd_ref, rot_ref, wq_ref, wu_ref, wo_ref, wd_ref,
                 out_ref, wq1, wu1, wo1, wd1,
-                wq, wu, wo, wd, xg, xg1, a_buf, m_buf, act, ctx, part, hop_a, hop_b, fin, vec_in, bias_in, vec, bq, bu,
+                wq, wu, wo, wd, xg, xg1, a_buf, m_buf, act, ctx, part, hop_a, hop_b, fin, vec_own, bias_own, bq_pad, vec_in, bias_in, vec, bq, bu,
                 v_ss, v_rs, b_ss, b_rs, x_ss, x_rs, a_ss, a_rs, w_ss, w_rs, c_ss, c_rs, r_ss, r_rs, loc, loc1):
     f32, bf = jnp.float32, jnp.bfloat16
     place = Place(side)
@@ -166,6 +172,33 @@
     right, left = place.in_row(1), place.in_row(-1)
     nxt, prv, far = place.step(place.col, 1), place.step(place.col, -1), place.step(place.col, 2)
 
+    second = place.core == 1
+    width = head // CORES
+    vec_own[...] = jnp.zeros_like(vec_own)
+    for layer in range(2):
+        vec_own[layer * 4:layer * 4 + 4, :width] = ln_ref[layer]
+    vec_own[8:10, :width] = bo_ref[...].astype(f32)
+    vec_own[10:12, :width] = bd_ref[...].astype(f32)
+    vec_own[12:13, :width] = jnp.full((1, width), lens_ref[0].astype(f32))
+    rows = vec_own[...]
+    vec_own[...] = jnp.where(second, pltpu.roll(rows, width, 1), rows)
+    bq_pad[...] = jnp.zeros_like(bq_pad)
+    bq_pad[:, :3 * width] = bq_ref[...].astype(f32)
+    lead, rest = bq_pad[:, :head], bq_pad[:, head:]
+    lead_turned, rest_turned = pltpu.roll(lead, width, 1), pltpu.roll(rest, width, 1)
+    upper = lax.broadcasted_iota(jnp.int32, lead.shape, 1) >= width
+    q_tiles = (jnp.where(second, 0.0, lead), jnp.where(second, jnp.where(upper, lead_turned, 0.0), rest),
+               jnp.where(second, jnp.where(upper, rest_turned, lead_turned), 0.0))
+    tiles = wide // head
+    bias_own[...] = jnp.zeros_like(bias_own)
+    for layer in range(2):
+        for t in range(3):
+            bias_own[layer * 3 + t:layer * 3 + t + 1, :] = q_tiles[t][layer:layer + 1]
+        for t in range(tiles):
+            t_core, t_at = t // (tiles // CORES), t % (tiles // CORES)
+            part_of = bu_ref[layer:layer + 1, t_at * head:(t_at + 1) * head].astype(f32)
+            bias_own[6 + layer * tiles + t:7 + layer * tiles + t, :] = jnp.where(place.core == t_core, part_of, 0.0)
+
     barrier = pltpu.get_barrier_semaphore()
     others = [lax.rem(place.me + d, count) for d in range(1, count)]
     for dev in others:
@@ -176,13 +209,10 @@
         for d in (1, 3, 2, 0):
             col = place.step(place.col, d)
             dst = dst_buf.at[place.row, place.col, place.core]
-            pairs = [(wq_ref.at[layer, col], dst)]
-            if kind:
-                pairs = []
-                for k in range(side):
-                    off = pl.multiple_of((k * side + col) * wide, wide)
-                    pairs.append((wu_ref.at[layer, :, pl.ds(off, wide)], dst.at[:, pl.ds(k * wide, wide)]))
-            for src, to in pairs:
+            src_ref, size = (wu_ref, wide) if kind else (wq_ref, triple)
+            for k in range(side):
+                off = pl.multiple_of((k * side + col) * size, size)
+                src, to = src_ref.at[layer, :, pl.ds(off, size)], dst.at[:, pl.ds(k * size, size)]
                 if d:
                     send(src, to, a_ss.at[layer, kind, d], a_rs.at[layer, kind, d], place.in_row(d))
                 else:
@@ -200,35 +230,39 @@
     gq1, gu1, go1, *gd1 = gathers[1]
     d_cols = wd.shape[4]
     rows_of = lambda ref, col, h: ref.at[col, pl.ds(h * half, half)]
-    x_ring = Ring(place, place.col, right, left, lambda col, h: rows_of(xg, col, h), lambda h: x_ref.at[pl.ds(h * half, half)], x_ss.at[0], x_rs.at[0])
-    x1_ring = Ring(place, place.col, right, left, lambda col, h: rows_of(xg1, col, h), lambda h: rows_of(xg1, place.col, h), x_ss.at[1], x_rs.at[1])
+    x_ring = Ring(place, place.col, right, left, lambda col, h: rows_of(xg, col, h), lambda h: x_ref.at[pl.ds(h * half, half)], x_ss.at[0, 0], x_rs.at[0, 0])
+    x1_at = lambda h: lambda col, half_at: xg1.at[col, pl.ds(half_at * half, half), pl.ds(h * d_cols, d_cols)]
+    x1_rings = [Ring(place, place.col, right, left, x1_at(h), lambda half_at, h=h: x1_at(h)(place.col, half_at), x_ss.at[1, h], x_rs.at[1, h]) for h in range(2)]
 
     exchange(0, 0, wq)
     vec_at = lambda core, chip: vec_in.at[core, :, pl.ds(pl.multiple_of(chip * head, head), head)]
     bias_at = lambda core, row: bias_in.at[core, :, pl.ds(pl.multiple_of(row * head, head), head)]
     for d, dev in enumerate(others):
-        send(vec_ref, vec_at(place.core, place.chip), v_ss.at[d], v_rs.at[d], dev)
+        send(vec_own, vec_at(place.core, place.chip), v_ss.at[d], v_rs.at[d], dev)
     column = [(e, c) for e in range(side) for c in range(CORES) if e or c]
     for i, (e, c) in enumerate(column):
         dev = place.dev(place.step(place.row, e), place.col, lax.rem(place.core + c, CORES))
-        send(bias_ref, bias_at(place.core, place.row), b_ss.at[i], b_rs.at[i], dev)
+        send(bias_own, bias_at(place.core, place.row), b_ss.at[i], b_rs.at[i], dev)
     exchange(0, 1, wu)
-    go.start()
-    gd[1].start()
+    for g in (go, gd[1]):
+        g.start()
+        g.own()
     x_ring.start()
     own = [(x_ref, xg.at[place.col]), (wo_ref.at[0], wo.at[place.row, place.core]), (wo_ref.at[1], wo1.at[place.row, place.core])]
     own += [(wd_ref.at[layer, :, pl.ds(h * d_cols, d_cols)], buf.at[h, place.row, place.core]) for layer, buf in enumerate((wd, wd1)) for h in range(2)]
     for i, (src, dst) in enumerate(own):
         pltpu.make_async_copy(src, dst, loc.at[i]).start()
 
-    vec_in[place.core, :, pl.ds(pl.multiple_of(place.chip * head, head), head)] = vec_ref[...]
-    bias_in[place.core, :, pl.ds(pl.multiple_of(place.row * head, head), head)] = bias_ref[...]
+    vec_in[place.core, :, pl.ds(pl.multiple_of(place.chip * head, head), head)] = vec_own[...]
+    bias_in[place.core, :, pl.ds(pl.multiple_of(place.row * head, head), head)] = bias_own[...]
 
     exchanged(0, 0, wq)
     gq.start()
+    gq.own()
     exchanged(0, 1, wu)
     gq.forward()
     gu.start()
+    gu.own()
 
     for d in range(1, count):
         src = lax.rem(place.me + count - d, count)
@@ -239,35 +273,34 @@
     for layer in range(2):
         for row in range(side):
             at = pl.ds(row * head, head)
-            for t in range(3):
-                i = layer * 3 + t
-                bq[layer:layer + 1, row * triple + t * head:row * triple + (t + 1) * head] = bias_in[0, i:i + 1, at] + bias_in[1, i:i + 1, at]
-            tiles = wide // head
-            for t in range(tiles):
-                i = 6 + layer * tiles + t
-                bu[layer:layer + 1, row * wide + t * head:row * wide + (t + 1) * head] = bias_in[0, i:i + 1, at] + bias_in[1, i:i + 1, at]
+            rows = bias_in[0, :, at] + bias_in[1, :, at]
+            for tall, out, first, n in ((triple, bq, 0, 3), (wide, bu, 6, tiles)):
+                for t in range(n):
+                    i = first + layer * n + t
+                    out[layer:layer + 1, row * tall + t * head:row * tall + (t + 1) * head] = rows[i:i + 1]
 
     x_ring.forward()
     exchange(1, 0, wq1)
     exchange(1, 1, wu1)
     go.forward()
+    gq.hand()
 
     tile = min(32, half)
 
-    def norm(src, doc, layer):
+    def norm(src, doc, layer, to, halves=(0, 1)):
         par = [vec[layer * 4 + i:layer * 4 + i + 1, :] for i in range(4)]
 
-        @pl.loop(0, seq, step=tile)
+        @pl.loop(halves[0] * half, (halves[-1] + 1) * half, step=tile)
         def _(r):
             at = pl.ds(r, tile)
             rows = src[doc, at, :].astype(f32)
             centered = rows - jnp.mean(rows, axis=-1, keepdims=True)
             var = jnp.mean(centered * centered, axis=-1, keepdims=True)
             normed = centered * lax.rsqrt(var + LN_EPS)
-            a_buf[at, :] = (normed * par[0] + par[1]).astype(bf)
+            to[at, :] = (normed * par[0] + par[1]).astype(bf)
             m_buf[doc, at, :] = (normed * par[2] + par[3]).astype(bf)
 
-    def attend(doc, layer):
+    def attend(doc, layer, rows):
         chip = place.row * side + doc
         lens = vec[12:13, pl.ds(pl.multiple_of(chip * head, head), head)]
         lane = lax.broadcasted_iota(jnp.int32, (1, head), 1)
@@ -286,7 +319,7 @@
         def _(p):
             at = pl.ds(pl.multiple_of(p * pair, pair), pair)
             w = wq[:, :, :, :, at].reshape(d_model, pair)
-            qkv = (jnp.dot(a_buf[...], w, preferred_element_type=f32) + bq[layer:layer + 1, at]).astype(bf)
+            qkv = (jnp.dot(rows[...], w, preferred_element_type=f32) + bq[layer:layer + 1, at]).astype(bf)
             for h in range(2):
                 q, k, v = (qkv[:, h * triple + j * head:h * triple + (j + 1) * head] for j in range(3))
                 scores = lax.dot_general(turn(q), turn(k), (((1,), (1,)), ((), ())), preferred_element_type=f32) * (head ** -0.5)
@@ -316,15 +349,18 @@
 
     top, low = pl.ds(0, half), pl.ds(half, half)
 
+    def send_part(layer, h, i, doc, rows, to, dev):
+        send(part.at[doc, h, rows], to.at[h], r_ss.at[layer, h, i], r_rs.at[layer, h, i], dev)
+
     def send_far(layer, h):
-        send(part.at[far, h, top], hop_a.at[h], r_ss.at[layer, h, 0], r_rs.at[layer, h, 0], left)
-        send(part.at[far, h, low], hop_b.at[h], r_ss.at[layer, h, 1], r_rs.at[layer, h, 1], right)
+        send_part(layer, h, 0, far, top, hop_a, left)
+        send_part(layer, h, 1, far, low, hop_b, right)
 
     def send_prv(layer, h):
-        send(part.at[prv, h, low], fin.at[0, h], r_ss.at[layer, h, 2], r_rs.at[layer, h, 2], left)
+        send_part(layer, h, 2, prv, low, fin.at[0], left)
 
     def send_nxt(layer, h):
-        send(part.at[nxt, h, top], fin.at[1, h], r_ss.at[layer, h, 3], r_rs.at[layer, h, 3], right)
+        send_part(layer, h, 3, nxt, top, fin.at[1], right)
 
     def pass_on(layer, h):
         for i, hop, doc, first, dev in ((0, hop_a, prv, 0, left), (1, hop_b, nxt, half, right)):
@@ -336,7 +372,7 @@
 
             send(hop.at[h], fin.at[2 + i, h], r_ss.at[layer, h, 4 + i], r_rs.at[layer, h, 4 + i], dev)
 
-    def owner_sums(layer, src, store):
+    def owner_sums(layer, src, store, done):
         for h in range(2):
             cols = slice(h * d_cols, (h + 1) * d_cols)
             for i in range(2, 6):
@@ -349,20 +385,30 @@
                     bias = vec[8 + layer:9 + layer, cols] + vec[10 + layer:11 + layer, cols]
                     store(at, cols, (src[place.col, at, cols].astype(f32) + (tot + bias)).astype(bf))
 
+            done(h)
+
     def sums_sent(layer):
         for h in range(2):
             for i in range(6):
                 settle(hop_a.at[h], r_ss.at[layer, h, i])
 
-    def nearest_first(i):
-        return lax.rem(place.col + jnp.where(i == 0, 0, jnp.where(i == 1, 1, jnp.where(i == 2, side - 1, 2))), side)
+    def chosen(i, docs):
+        doc = docs[-1]
+        for at, other in enumerate(docs[:-1]):
+            doc = jnp.where(i == at, other, doc)
+        return doc
+
+    mine = place.col
+    nearest_first = (mine, nxt, prv, far)
+    farthest_first = (far, nxt, prv, mine)
 
     settle(xg.at[place.col], loc.at[0])
-    gq.finish()
+    gq.tail()
+    gq.take()
 
     @pl.loop(0, side)
     def _(i):
-        doc = nearest_first(i)
+        doc = chosen(i, nearest_first)
 
         @pl.when(i == 1)
         def _():
@@ -372,15 +418,21 @@
         def _():
             gu.forward()
             gd[0].start()
+            gd[0].own()
+            go.hand()
 
         @pl.when(i == 3)
         def _():
             x_ring.last()
-
-        norm(xg, doc, 0)
-        attend(doc, 0)
-
-    gu.finish()
+            gu.hand()
+
+        norm(xg, doc, 0, a_buf)
+        attend(doc, 0, a_buf)
+
+    gd[1].hand()
+    go.tail()
+    gu.tail()
+    gu.take()
 
     @pl.loop(0, side)
     def _(doc):
@@ -391,23 +443,25 @@
             gd[0].forward()
             gd[1].forward()
 
-        @pl.when(doc == 1)
-        def _():
-            exchanged(1, 0, wq1)
-            exchanged(1, 1, wu1)
-            gq1.start()
-            gu1.start()
-
-    go.finish()
+        @pl.when(doc == 2)
+        def _():
+            gd[0].hand()
+
+    gd[0].tail()
+    exchanged(1, 0, wq1)
+    exchanged(1, 1, wu1)
+    gq1.start()
+    gu1.start()
     settle(wo.at[place.row, place.core], loc.at[1])
+    go.take()
 
     for h in range(2):
         settle(wd.at[h, place.row, place.core], loc.at[3 + h])
-        gd[h].finish()
+        gd[h].take()
 
         @pl.loop(0, side)
         def _(i, h=h):
-            doc = lax.rem(place.col + jnp.where(i == 0, 2, jnp.where(i == 1, 1, jnp.where(i == 2, side - 1, 0))), side)
+            doc = chosen(i, farthest_first)
             down(doc, h)
 
             @pl.when(i == 0)
@@ -417,75 +471,105 @@
             @pl.when(i == 1)
             def _():
                 send_nxt(0, h)
+                if h == 0:
+                    gd[1].tail()
 
             @pl.when(i == 2)
             def _():
                 send_prv(0, h)
 
+    gq1.own()
+    gu1.own()
     gq1.forward()
     pass_on(0, 0)
+    gu1.forward()
+    for g in (go1, *gd1):
+        g.start()
+        g.own()
     pass_on(0, 1)
-    gu1.forward()
-    go1.start()
-    gd1[0].start()
-    gd1[1].start()
     for g in gathers[0]:
         g.drain()
-    gq1.finish()
+    gq1.hand()
+    gq1.tail()
+    gu1.hand()
+    gq1.take()
     pltpu.make_async_copy(wq1, wq, loc1.at[0]).start()
-    gu1.finish()
+    gu1.tail()
+    gu1.take()
     pltpu.make_async_copy(wu1, wu, loc1.at[1]).start()
 
     def keep(at, cols, rows):
         xg1[place.col, at, cols] = rows
 
-    owner_sums(0, xg, keep)
-    x1_ring.start()
+    owner_sums(0, xg, keep, lambda h: x1_rings[h].start())
     go1.forward()
+    gd1[0].forward()
     sums_sent(0)
+    x_ring.drain()
     settle(wq, loc1.at[0])
     settle(wu, loc1.at[1])
 
+    norm(xg1, place.col, 1, xg.at[place.col])
+
     @pl.loop(0, side)
     def _(i):
-        doc = nearest_first(i)
+        doc = chosen(i, nearest_first)
 
         @pl.when(i == 1)
         def _():
-            x1_ring.rest()
+            for ring in x1_rings:
+                ring.rest()
+            norm(xg1, nxt, 1, xg.at[nxt], (0,))
+
+        @pl.when(i == 3)
+        def _():
+            for ring in x1_rings:
+                ring.last()
+            norm(xg1, far, 1, xg.at[far])
+
+        attend(doc, 1, xg.at[doc])
+
+        @pl.when(i == 1)
+        def _():
+            gd1[0].tail()
+            gd1[1].hand()
 
         @pl.when(i == 2)
         def _():
+            gd1[1].tail()
+
+        up(doc, 1)
+
+        @pl.when(i == 0)
+        def _():
+            for ring in x1_rings:
+                ring.forward()
+            gd1[1].forward()
+            norm(xg1, nxt, 1, xg.at[nxt], (1,))
+            norm(xg1, prv, 1, xg.at[prv], (0,))
+            go1.hand()
+            gd1[0].hand()
+            go1.tail()
             settle(wo1.at[place.row, place.core], loc.at[2])
-            go1.finish()
+            go1.take()
             pltpu.make_async_copy(wo1, wo, loc1.at[2]).start()
+
+        @pl.when(i == 1)
+        def _():
             settle(wd1.at[0, place.row, place.core], loc.at[5])
-            gd1[0].finish()
+            gd1[0].take()
             pltpu.make_async_copy(wd1.at[0], wd.at[0], loc1.at[3]).start()
-
-        @pl.when(i == 3)
-        def _():
-            x1_ring.last()
-
-        norm(xg1, doc, 1)
-        attend(doc, 1)
-        up(doc, 1)
-
-        @pl.when(i == 0)
-        def _():
-            x1_ring.forward()
-            gd1[0].forward()
-            gd1[1].forward()
-
-        @pl.when(i == 2)
-        def _():
-            settle(wd1.at[1, place.row, place.core], loc.at[6])
-            gd1[1].finish()
-            pltpu.make_async_copy(wd1.at[1], wd.at[1], loc1.at[4]).start()
+            norm(xg1, prv, 1, xg.at[prv], (1,))
             settle(wo, loc1.at[2])
             settle(wd.at[0], loc1.at[3])
             down(nxt, 0)
             send_nxt(1, 0)
+
+        @pl.when(i == 2)
+        def _():
+            settle(wd1.at[1, place.row, place.core], loc.at[6])
+            gd1[1].take()
+            pltpu.make_async_copy(wd1.at[1], wd.at[1], loc1.at[4]).start()
             down(prv, 0)
             send_prv(1, 0)
             settle(wd.at[1], loc1.at[4])
@@ -508,16 +592,16 @@
     def give_out(at, cols, rows):
         out_ref[at, cols] = rows
 
-    owner_sums(1, xg1, give_out)
+    owner_sums(1, xg1, give_out, lambda h: None)
     sums_sent(1)
     for g in gathers[1]:
         g.drain()
-    x_ring.drain()
-    x1_ring.drain()
+    for ring in x1_rings:
+        ring.drain()
     for d in range(count - 1):
-        settle(vec_ref, v_ss.at[d])
+        settle(vec_own, v_ss.at[d])
     for i in range(len(column)):
-        settle(bias_ref, b_ss.at[i])
+        settle(bias_own, b_ss.at[i])
     for layer in range(2):
         for kind, buf in enumerate((wq, wu)):
             for d in range(1, side):
@@ -530,8 +614,9 @@
 
 
 def solution(mesh):
-    row_spec = P(('dp', 'fsdp'), None, None)
-    in_specs = (row_spec, P(('dp', 'fsdp')), P(None, None, 'fsdp'), P(None, 'fsdp', None, None), P(None, 'fsdp'), P(None, 'fsdp', None), P(None, 'fsdp'), P(None, 'fsdp', None), P(None, 'fsdp'), P(None, 'fsdp', None), P(None, 'fsdp'))
+    row_spec = P(('dp', 'fsdp'))
+    inner = P(None, 'fsdp')
+    in_specs = (row_spec, P(('dp', 'fsdp')), P(None, *inner)) + (inner,) * len(('w_qkv', 'b_qkv', 'w_out', 'b_out', 'w_up', 'b_up', 'w_down', 'b_down'))
     count = mesh.shape['fsdp']
     side = math.isqrt(count // CORES)
 
@@ -544,18 +629,8 @@
         ff_rows = w_down.shape[1]
         ff = ff_rows * CORES * side
         bf, f32 = jnp.bfloat16, jnp.float32
-        core = lax.axis_index('fsdp') % CORES
-
-        def placed(vals):
-            zero = jnp.zeros_like(vals)
-            return jnp.where(core == 0, jnp.concatenate([vals, zero], axis=-1), jnp.concatenate([zero, vals], axis=-1))
-
-        lens_row = jnp.broadcast_to(lens_loc.astype(f32)[:, None], (1, d_rows))
-        vec = jnp.concatenate([ln_par.reshape(-1, d_rows), b_out.astype(f32), b_down.astype(f32), lens_row, jnp.zeros((3, d_rows), f32)], axis=0)
-        vec = placed(vec)
-        bias = jnp.concatenate([placed(b_qkv.astype(f32)).reshape(-1, head_dim), placed(b_up.astype(f32)).reshape(-1, head_dim)], axis=0)
-        bias = jnp.pad(bias, ((0, -bias.shape[0] % 16), (0, 0)))
-        wq = w_qkv.reshape(layers, d_rows, per, side, triple).transpose(0, 3, 1, 2, 4).reshape(layers, side, d_rows, per * triple)
+        wq = w_qkv.reshape(layers, d_rows, heads * triple)
+        bias_rows = -(-layers * (3 + ff // side // head_dim) // 16) * 16
 
         half = seq_len // 2
         wq_s, wu_s = (side, side, CORES, d_rows, per * triple), (side, side, CORES, d_rows, ff)
@@ -563,7 +638,7 @@
         outs = pl.pallas_call(
             functools.partial(both_layers, side),
             out_shape=(jax.ShapeDtypeStruct((seq_len, d_model), bf), *(jax.ShapeDtypeStruct(s, bf) for s in (wq_s, wu_s, wo_s, wd_s))),
-            in_specs=[ANY, VM, VM, VM, ANY, ANY, ANY, ANY],
+            in_specs=[ANY, pl.BlockSpec(memory_space=pltpu.SMEM), VM, VM, VM, VM, VM, VM, ANY, ANY, ANY, ANY],
             out_specs=(VM, ANY, ANY, ANY, ANY),
             scratch_shapes=[
                 *(pltpu.VMEM(s, bf) for s in (wq_s, wu_s, wo_s, wd_s)),
@@ -577,18 +652,21 @@
                 pltpu.VMEM((2, half, d_model // 2), f32),
                 pltpu.VMEM((2, half, d_model // 2), f32),
                 pltpu.VMEM((4, 2, half, d_model // 2), f32),
+                pltpu.VMEM((16, head_dim), f32),
+                pltpu.VMEM((bias_rows, head_dim), f32),
+                pltpu.VMEM((layers, 2 * head_dim), f32),
                 pltpu.VMEM((CORES, 16, d_model), f32),
-                pltpu.VMEM((CORES, bias.shape[0], side * head_dim), f32),
+                pltpu.VMEM((CORES, bias_rows, side * head_dim), f32),
                 pltpu.VMEM((16, d_model), f32),
                 pltpu.VMEM((layers, per * triple), f32),
                 pltpu.VMEM((layers, ff), f32),
-                DMA((count - 1,)), DMA((count - 1,)), DMA((side * CORES - 1,)), DMA((side * CORES - 1,)),
-                DMA((2, 6)), DMA((2, 6)), DMA((2, 2, side)), DMA((2, 2, side)),
-                DMA((2, 5, 6)), DMA((2, 5, 6)), DMA((2, 5, 8)), DMA((2, 5, 8)),
-                DMA((2, 2, 6)), DMA((2, 2, 6)), DMA((7,)), DMA((5,)),
+                *([DMA((count - 1,))] * 2), *([DMA((side * CORES - 1,))] * 2),
+                *([DMA((layers, 2, 6))] * 2), *([DMA((layers, 2, side))] * 2),
+                *([DMA((layers, 5, 6))] * 2), *([DMA((layers, 5, 8))] * 2),
+                *([DMA((layers, 2, 6))] * 2), DMA((7,)), DMA((5,)),
             ],
             compiler_params=pltpu.CompilerParams(collective_id=0, has_side_effects=True, vmem_limit_bytes=67043328),
-        )(hidden_loc[0], vec, bias, rotary_factors(seq_len, head_dim), wq, w_up, w_out, w_down)
+        )(hidden_loc[0], lens_loc, ln_par, b_qkv, b_out, b_up, b_down, rotary_factors(seq_len, head_dim), wq, w_up, w_out, w_down)
         return outs[0][None]
 
     return jax.shard_map(local_step, mesh=mesh, in_specs=in_specs, out_specs=row_spec, check_vma=False)

time: 322 us -> 310 us (0.963)
  Pallas kernels: 310 us -> 303 us
    pallas_call x1, Pallas kernels: 310 us -> 303 us  [local_step(): pl.pallas_call(functools.partial(both_layers, side), out_shape=(jax.Shape...]
where the time goes in v4:
time: 310 us; the launch traced here: 309 us
  Pallas kernels  303 us (98%)
  local copies, waits for them, and re-layouts  5.88 us (2%)
    pallas_call x1, Pallas kernels, local_step(): pl.pallas_call(functools.partial(both_layers, side), out_shape=(jax.Shape...  303 us

profile of v4, /device:TPU:97, one launch (start us, length us, event | category | flops | bytes accessed | tf_op | source)
XLA Modules:
  0.0 309.3 jit_solution(9073949765542168773)
XLA Ops:
  0.7 3.6 %reshape.3.wq_ref = bf16[2,64,6144]{2,1,0:T(8,128)(2,1)} reshape(bf16[2,64,16,384]{3,2,1,0:T(8,128)(2,1)} %param.15) | data formatting | bytes 3145728 | tf_op jit(solution)/shard_map/reshape | solution.py:632
  4.2 302.8 %shard_map.118 = (bf16[256,2048]{1,0:T(8,128)(2,1)}, bf16[4,4,2,64,1536]{4,3,2,1,0:T(8,128)(2,1)}, bf16[4,4,2,64,2048]{4,3,2,1,0:T(8,128)(2,1)}, bf16[4,2,64,204...) custom-call(bf16[256,2048]{1,0:T(8,128)(2,1)} %bitcast.5, s32[1]{0:T(128)S(6)} %copy.14.lens_ref, f32[2,4,64]{2,1,0:T(4,128)} %ln_ref.1, ...), custom_call_target="tpu_custom_call" | custom-call | tf_op jit(solution)/shard_map/pallas_call | solution.py:638
  307.0 2.3 copy.15

commit v5 on v4

--- a/solution.py
+++ b/solution.py
@@ -157,8 +157,8 @@
 
 def both_layers(side, x_ref, lens_ref, ln_ref, bq_ref, bo_ref, bu_ref, bd_ref, rot_ref, wq_ref, wu_ref, wo_ref, wd_ref,
                 out_ref, wq1, wu1, wo1, wd1,
-                wq, wu, wo, wd, xg, xg1, a_buf, m_buf, act, ctx, part, hop_a, hop_b, fin, vec_own, bias_own, bq_pad, vec_in, bias_in, vec, bq, bu,
-                v_ss, v_rs, b_ss, b_rs, x_ss, x_rs, a_ss, a_rs, w_ss, w_rs, c_ss, c_rs, r_ss, r_rs, loc, loc1):
+                wq, wu, wo, wd, xg, xg1, a_buf, m_buf, act, ctx, part, hop_a, hop_b, fin, q_stage, u_stage, q_own, u_own, vec_own, bias_own, bq_pad, vec_in, bias_in, vec, bq, bu,
+                v_ss, v_rs, b_ss, b_rs, x_ss, x_rs, a_ss, a_rs, e_ss, e_rs, w_ss, w_rs, c_ss, c_rs, r_ss, r_rs, loc, loc1):
     f32, bf = jnp.float32, jnp.bfloat16
     place = Place(side)
     count = side * side * CORES
@@ -205,18 +205,35 @@
         pl.semaphore_signal(barrier, inc=1, device_id={"fsdp": dev}, device_id_type=MESH)
     pl.semaphore_wait(barrier, count - 1)
 
+    stages, own_stages = (q_stage, u_stage), (q_own, u_own)
+
     def exchange(layer, kind, dst_buf):
+        src_ref, size = (wu_ref, wide) if kind else (wq_ref, triple)
         for d in (1, 3, 2, 0):
             col = place.step(place.col, d)
             dst = dst_buf.at[place.row, place.col, place.core]
-            src_ref, size = (wu_ref, wide) if kind else (wq_ref, triple)
             for k in range(side):
                 off = pl.multiple_of((k * side + col) * size, size)
                 src, to = src_ref.at[layer, :, pl.ds(off, size)], dst.at[:, pl.ds(k * size, size)]
-                if d:
+                if d == 2:
+                    way, at = k // 2, pl.ds(k % 2 * size, size)
+                    send(src, stages[kind].at[layer, way, :, at], e_ss.at[layer, kind, way], e_rs.at[layer, kind, way], (right, left)[way])
+                elif d:
                     send(src, to, a_ss.at[layer, kind, d], a_rs.at[layer, kind, d], place.in_row(d))
+                elif layer:
+                    pltpu.make_async_copy(src, own_stages[kind].at[:, pl.ds(k * size, size)], loc.at[4 + kind]).start()
                 else:
                     pltpu.make_async_copy(src, to, a_rs.at[layer, kind, d]).start()
+
+    def relay(layer, kind, dst_buf):
+        for way, (origin, dev) in enumerate(((prv, right), (nxt, left))):
+            piece = stages[kind].at[layer, way]
+            settle(piece, e_rs.at[layer, kind, way])
+            to = dst_buf.at[place.row, origin, place.core, :, pl.ds(way * piece.shape[1], piece.shape[1])]
+            send(piece, to, a_ss.at[layer, kind, 2], a_rs.at[layer, kind, 2], dev)
+        if layer:
+            settle(own_stages[kind], loc.at[4 + kind])
+            pltpu.make_async_copy(own_stages[kind], dst_buf.at[place.row, place.col, place.core], a_rs.at[layer, kind, 0]).start()
 
     def exchanged(layer, kind, dst_buf):
         for d in range(side):
@@ -243,13 +260,13 @@
     for i, (e, c) in enumerate(column):
         dev = place.dev(place.step(place.row, e), place.col, lax.rem(place.core + c, CORES))
         send(bias_own, bias_at(place.core, place.row), b_ss.at[i], b_rs.at[i], dev)
-    exchange(0, 1, wu)
-    for g in (go, gd[1]):
+    for g in (go, gd[0]):
         g.start()
         g.own()
-    x_ring.start()
-    own = [(x_ref, xg.at[place.col]), (wo_ref.at[0], wo.at[place.row, place.core]), (wo_ref.at[1], wo1.at[place.row, place.core])]
-    own += [(wd_ref.at[layer, :, pl.ds(h * d_cols, d_cols)], buf.at[h, place.row, place.core]) for layer, buf in enumerate((wd, wd1)) for h in range(2)]
+    relay(0, 0, wq)
+    exchange(0, 1, wu)
+    own = [(x_ref, xg.at[place.col]), (wo_ref.at[0], wo.at[place.row, place.core])]
+    own += [(wd_ref.at[0, :, pl.ds(h * d_cols, d_cols)], wd.at[h, place.row, place.core]) for h in range(2)]
     for i, (src, dst) in enumerate(own):
         pltpu.make_async_copy(src, dst, loc.at[i]).start()
 
@@ -259,6 +276,8 @@
     exchanged(0, 0, wq)
     gq.start()
     gq.own()
+    relay(0, 1, wu)
+    x_ring.start()
     exchanged(0, 1, wu)
     gq.forward()
     gu.start()
@@ -417,73 +436,75 @@
         @pl.when(i == 2)
         def _():
             gu.forward()
-            gd[0].start()
-            gd[0].own()
+            gd[0].forward()
+            gd[1].start()
+            gd[1].own()
             go.hand()
 
         @pl.when(i == 3)
         def _():
             x_ring.last()
+            relay(1, 0, wq1)
+            relay(1, 1, wu1)
             gu.hand()
+            gd[0].hand()
 
         norm(xg, doc, 0, a_buf)
         attend(doc, 0, a_buf)
 
-    gd[1].hand()
     go.tail()
     gu.tail()
     gu.take()
+    settle(wo.at[place.row, place.core], loc.at[1])
+    for h in range(2):
+        settle(wd.at[h, place.row, place.core], loc.at[2 + h])
+
+    def leave(i, h):
+        for at, out in enumerate((send_far, send_nxt, send_prv)):
+            @pl.when(i == at)
+            def _(out=out):
+                out(0, h)
 
     @pl.loop(0, side)
-    def _(doc):
+    def _(i):
+        doc = chosen(i, farthest_first)
         up(doc, 0)
 
-        @pl.when(doc == 0)
-        def _():
-            gd[0].forward()
+        @pl.when(i == 0)
+        def _():
+            gd[0].tail()
+            go.take()
+            gd[0].take()
+
+        down(doc, 0)
+        leave(i, 0)
+
+        @pl.when(i == 1)
+        def _():
             gd[1].forward()
-
-        @pl.when(doc == 2)
-        def _():
-            gd[0].hand()
-
-    gd[0].tail()
-    exchanged(1, 0, wq1)
-    exchanged(1, 1, wu1)
-    gq1.start()
-    gu1.start()
-    settle(wo.at[place.row, place.core], loc.at[1])
-    go.take()
-
-    for h in range(2):
-        settle(wd.at[h, place.row, place.core], loc.at[3 + h])
-        gd[h].take()
-
-        @pl.loop(0, side)
-        def _(i, h=h):
-            doc = chosen(i, farthest_first)
-            down(doc, h)
-
-            @pl.when(i == 0)
-            def _():
-                send_far(0, h)
-
-            @pl.when(i == 1)
-            def _():
-                send_nxt(0, h)
-                if h == 0:
-                    gd[1].tail()
-
-            @pl.when(i == 2)
-            def _():
-                send_prv(0, h)
+            exchanged(1, 0, wq1)
+            gq1.start()
+
+        @pl.when(i == 2)
+        def _():
+            exchanged(1, 1, wu1)
+            gu1.start()
+            gd[1].hand()
+
+    gd[1].tail()
+    gd[1].take()
+
+    @pl.loop(0, side)
+    def _(i):
+        down(chosen(i, farthest_first), 1)
+        leave(i, 1)
 
     gq1.own()
     gu1.own()
     gq1.forward()
     pass_on(0, 0)
     gu1.forward()
-    for g in (go1, *gd1):
+    for g in (go1, gd1[0]):
         g.start()
         g.own()
     pass_on(0, 1)
@@ -502,13 +523,20 @@
         xg1[place.col, at, cols] = rows
 
     owner_sums(0, xg, keep, lambda h: x1_rings[h].start())
-    go1.forward()
-    gd1[0].forward()
     sums_sent(0)
     x_ring.drain()
     settle(wq, loc1.at[0])
     settle(wu, loc1.at[1])
 
+    def load_rows(src, dst, own_src, sem):
+        for e in range(side):
+            for c in range(CORES):
+                at = (place.step(place.row, e), lax.rem(place.core + c, CORES))
+                pltpu.make_async_copy(src.at[at] if e or c else own_src, dst.at[at], sem).start()
+
+    def load_down(h):
+        load_rows(wd1.at[h], wd.at[h], wd_ref.at[1, :, pl.ds(h * d_cols, d_cols)], loc1.at[3 + h])
+
     norm(xg1, place.col, 1, xg.at[place.col])
 
     @pl.loop(0, side)
@@ -531,45 +559,45 @@
 
         @pl.when(i == 1)
         def _():
-            gd1[0].tail()
+            for g in (go1, gd1[0]):
+                g.hand()
+                g.tail()
+
+        @pl.when(i == 2)
+        def _():
             gd1[1].hand()
-
-        @pl.when(i == 2)
-        def _():
             gd1[1].tail()
 
         up(doc, 1)
 
         @pl.when(i == 0)
         def _():
+            go1.forward()
+            gd1[0].forward()
+            gd1[1].start()
+            gd1[1].own()
             for ring in x1_rings:
                 ring.forward()
-            gd1[1].forward()
             norm(xg1, nxt, 1, xg.at[nxt], (1,))
             norm(xg1, prv, 1, xg.at[prv], (0,))
-            go1.hand()
-            gd1[0].hand()
-            go1.tail()
-            settle(wo1.at[place.row, place.core], loc.at[2])
+
+        @pl.when(i == 1)
+        def _():
             go1.take()
-            pltpu.make_async_copy(wo1, wo, loc1.at[2]).start()
-
-        @pl.when(i == 1)
-        def _():
-            settle(wd1.at[0, place.row, place.core], loc.at[5])
+            load_rows(wo1, wo, wo_ref.at[1], loc1.at[2])
             gd1[0].take()
-            pltpu.make_async_copy(wd1.at[0], wd.at[0], loc1.at[3]).start()
+            load_down(0)
             norm(xg1, prv, 1, xg.at[prv], (1,))
             settle(wo, loc1.at[2])
             settle(wd.at[0], loc1.at[3])
             down(nxt, 0)
             send_nxt(1, 0)
+            gd1[1].forward()
 
         @pl.when(i == 2)
         def _():
-            settle(wd1.at[1, place.row, place.core], loc.at[6])
             gd1[1].take()
-            pltpu.make_async_copy(wd1.at[1], wd.at[1], loc1.at[4]).start()
+            load_down(1)
             down(prv, 0)
             send_prv(1, 0)
             settle(wd.at[1], loc1.at[4])
@@ -606,6 +634,8 @@
         for kind, buf in enumerate((wq, wu)):
             for d in range(1, side):
                 settle(buf.at[0, 0, 0], a_ss.at[layer, kind, d])
+            for way in range(2):
+                settle(stages[kind].at[layer, way], e_ss.at[layer, kind, way])
 
 
 VM = pl.BlockSpec(memory_space=pltpu.VMEM)
@@ -652,6 +682,8 @@
                 pltpu.VMEM((2, half, d_model // 2), f32),
                 pltpu.VMEM((2, half, d_model // 2), f32),
                 pltpu.VMEM((4, 2, half, d_model // 2), f32),
+                *(pltpu.VMEM((layers, 2, d_rows, cols // 2), bf) for cols in (per * triple, ff)),
+                *(pltpu.VMEM((d_rows, cols), bf) for cols in (per * triple, ff)),
                 pltpu.VMEM((16, head_dim), f32),
                 pltpu.VMEM((bias_rows, head_dim), f32),
                 pltpu.VMEM((layers, 2 * head_dim), f32),
@@ -661,7 +693,7 @@
                 pltpu.VMEM((layers, per * triple), f32),
                 pltpu.VMEM((layers, ff), f32),
                 *([DMA((count - 1,))] * 2), *([DMA((side * CORES - 1,))] * 2),
-                *([DMA((layers, 2, 6))] * 2), *([DMA((layers, 2, side))] * 2),
+                *([DMA((layers, 2, 6))] * 2), *([DMA((layers, 2, side))] * 2), *([DMA((layers, 2, 2))] * 2),
                 *([DMA((layers, 5, 6))] * 2), *([DMA((layers, 5, 8))] * 2),
                 *([DMA((layers, 2, 6))] * 2), DMA((7,)), DMA((5,)),
             ],

time: 310 us -> 310 us (level)
  no operation moved by 1% of the time
where the time goes in v5:
time: 310 us
  Pallas kernels  303 us (98%)
  local copies, waits for them, and re-layouts  5.88 us (2%)
    pallas_call x1, Pallas kernels, local_step(): pl.pallas_call(functools.partial(both_layers, side), out_shape=(jax.Shape...  303 us

profile of v5, /device:TPU:97, one launch (start us, length us, event | category | flops | bytes accessed | tf_op | source)
XLA Modules:
  0.0 309.9 jit_solution(3685471708813482803)
XLA Ops:
  0.7 3.6 %reshape.3.wq_ref = bf16[2,64,6144]{2,1,0:T(8,128)(2,1)} reshape(bf16[2,64,16,384]{3,2,1,0:T(8,128)(2,1)} %param.15) | data formatting | bytes 3145728 | tf_op jit(solution)/shard_map/reshape | solution.py:662
  4.2 303.4 %shard_map.118 = (bf16[256,2048]{1,0:T(8,128)(2,1)}, bf16[4,4,2,64,1536]{4,3,2,1,0:T(8,128)(2,1)}, bf16[4,4,2,64,2048]{4,3,2,1,0:T(8,128)(2,1)}, bf16[4,2,64,204...) custom-call(bf16[256,2048]{1,0:T(8,128)(2,1)} %bitcast.5, s32[1]{0:T(128)S(6)} %copy.14.lens_ref, f32[2,4,64]{2,1,0:T(4,128)} %ln_ref.1, ...), custom_call_target="tpu_custom_call" | custom-call | tf_op jit(solution)/shard_map/pallas_call | solution.py:668
  307.6 2.3 copy.15
